TPU v7x, 32 devices: a whole 2x2x4 slice. The times are simulated.
32 devices in a mesh: dp: 8 (over z, x), tensor: 4 (over y, core).
Axes of the slice: x: 2, y: 2, z: 4, core: 2. Of those that a mesh axis runs over, the one named last changes fastest.
Arguments:
- hidden_in: bfloat16 [8, 256, 2048], P('dp'), may hold values from -6 to 6
- upstream_grad: bfloat16 [8, 256, 2048], P('dp'), may hold values from -6 to 6
- seq_lengths: int32 [8], replicated, may hold values from 1 to 256, 1536 in all
- position_order: int32 [8], replicated, may hold values from 0 to 7, each once
- query_weight: bfloat16 [2048, 2048], P(None, 'tensor'), may hold values from -0.125 to 0.125
- key_weight: bfloat16 [2048, 2048], P(None, 'tensor'), may hold values from -0.125 to 0.125
- value_weight: bfloat16 [2048, 2048], P(None, 'tensor'), may hold values from -0.125 to 0.125
- output_weight: bfloat16 [2048, 2048], P('tensor'), may hold values from -0.125 to 0.125
- query_gain: float32 [2048], P('tensor'), may hold values from 0.25 to 1.75
- key_gain: float32 [2048], P('tensor'), may hold values from 0.25 to 1.75
- attn_gain: float32 [2048], replicated, may hold values from 0.25 to 1.75
- gate_weight: bfloat16 [2048, 8192], P(None, 'tensor'), may hold values from -0.125 to 0.125
- up_weight: bfloat16 [2048, 8192], P(None, 'tensor'), may hold values from -0.125 to 0.125
- down_weight: bfloat16 [8192, 2048], P('tensor'), may hold values from -0.0625 to 0.0625
- mlp_gain: float32 [2048], replicated, may hold values from 0.25 to 1.75
Outputs:
- layer_out: bfloat16 [8, 256, 2048], P('dp')
- input_grad: bfloat16 [8, 256, 2048], P('dp')
- query_weight_grad: float32 [2048, 2048], P('dp', 'tensor')
- key_weight_grad: float32 [2048, 2048], P('dp', 'tensor')
- value_weight_grad: float32 [2048, 2048], P('dp', 'tensor')
- output_weight_grad: float32 [2048, 2048], P('tensor', 'dp')
- query_gain_grad: float32 [2048], P('tensor')
- key_gain_grad: float32 [2048], P('tensor')
- attn_gain_grad: float32 [2048], replicated
- gate_weight_grad: float32 [2048, 8192], P('dp', 'tensor')
- up_weight_grad: float32 [2048, 8192], P('dp', 'tensor')
- down_weight_grad: float32 [8192, 2048], P('tensor', 'dp')
- mlp_gain_grad: float32 [2048], replicated
- rms_values: float32 [3], replicated
Inputs may be any that keep to these rules, and one draw needn't show every extreme that they name: `seq_lengths`: lengths of the 8 sequences in sequence order; one is exactly 256; they sum to 1536. `position_order`: a permutation: every sequence sits at exactly one data position.
All inputs are finite; a program needn't handle non-finite values.
Results may differ from a plain program's by a relative error of at most 0.019.
Values may be sent and summed in bfloat16 or wider, within the bound.
A program may use at most 192 MiB of HBM per device.

v0:
```python
import math

import jax
import jax.numpy as jnp
from jax import lax
from jax.sharding import PartitionSpec as P

D = 2048
HEAD = 128


EPS = 1e-06


def matmul(left, right):
    return jnp.dot(left, right, preferred_element_type=jnp.float32)


def left_inner(left, right):
    return lax.dot_general(
        left, right, (((0,), (0,)), ((), ())), preferred_element_type=jnp.float32
    )


def right_inner(left, right):
    return lax.dot_general(
        left, right, (((1,), (1,)), ((), ())), preferred_element_type=jnp.float32
    )


def rope_tables(rows, width):
    places = jnp.arange(rows, dtype=jnp.float32)
    freq = jnp.power(
        jnp.float32(500000.0), -jnp.arange(width // 2, dtype=jnp.float32) * (2.0 / width)
    )
    angle = places[:, None] * freq[None, :]
    return (jnp.cos(angle), jnp.sin(angle))


def rotate(field, cosine, sine, sign):
    half = field.shape[-1] // 2
    first = field[..., :half]
    second = field[..., half:]
    cosine = cosine[:, None, :]
    sine = sine[:, None, :] * sign
    return jnp.concatenate(
        [first * cosine - second * sine, second * cosine + first * sine], axis=-1
    )


def deal_rows(pieces):
    return lax.all_to_all(pieces, "dp", split_axis=0, concat_axis=0, tiled=True)


def return_rows(pieces):
    return (
        lax.all_to_all(pieces[0], "dp", split_axis=0, concat_axis=0, tiled=True),
        lax.all_to_all(pieces[1], "dp", split_axis=0, concat_axis=0, tiled=True),
    )


def block_scores(query_block, keys, start, length):
    scores = jnp.einsum(
        "qhe,khe->hqk", query_block, keys, preferred_element_type=jnp.float32
    ) / math.sqrt(HEAD)
    query_ids = start + jnp.arange(query_block.shape[0], dtype=jnp.int32)
    key_ids = jnp.arange(keys.shape[0], dtype=jnp.int32)
    allowed = (key_ids[None, :] <= query_ids[:, None]) & (key_ids[None, :] < length)
    return jnp.where(allowed[None], scores, -1e30)


def post_norm_back(grad, unit, scale, gain):
    scaled = grad * gain
    return scale * (scaled - unit * jnp.mean(scaled * unit, axis=-1, keepdims=True))


def body(
    hidden_in,
    upstream_grad,
    seq_lengths,
    position_order,
    query_weight,
    key_weight,
    value_weight,
    output_weight,
    query_gain,
    key_gain,
    attn_gain,
    gate_weight,
    up_weight,
    down_weight,
    mlp_gain,
):
    count = lax.axis_size("dp")
    myself = lax.axis_index("dp")
    index = jnp.arange(count, dtype=jnp.int32)
    inverse = jnp.sum(
        index[None, :] * (position_order[None, :] == index[:, None]).astype(jnp.int32), axis=1
    )
    rows = hidden_in.shape[1]
    width = hidden_in.shape[2]
    piece = rows // count
    seq_here = jnp.sum(jnp.where(index == myself, position_order, 0))
    length = jnp.sum(jnp.where(index == seq_here, seq_lengths, 0))
    live = (jnp.arange(rows, dtype=jnp.int32) < length)[:, None]
    first = deal_rows(upstream_grad.reshape(count, piece, width))
    second = deal_rows(jnp.take(first, position_order, axis=0))
    grad_in = jnp.where(live, second.reshape(rows, width).astype(jnp.float32), 0.0)
    rows_low = hidden_in[0]
    rows_f = rows_low.astype(jnp.float32)
    local = query_weight.shape[1]
    heads_here = local // HEAD
    q_raw = matmul(rows_low, query_weight)
    k_raw = matmul(rows_low, key_weight)
    values = matmul(rows_low, value_weight).astype(jnp.bfloat16).reshape(rows, heads_here, HEAD)
    q_total, k_total = lax.psum(
        (jnp.sum(q_raw * q_raw, axis=-1), jnp.sum(k_raw * k_raw, axis=-1)), "tensor"
    )
    q_scale = lax.rsqrt(q_total / D + EPS)[:, None]
    k_scale = lax.rsqrt(k_total / D + EPS)[:, None]
    q_unit = q_raw * q_scale
    k_unit = k_raw * k_scale
    cosine, sine = rope_tables(rows, HEAD)
    queries = rotate(
        (q_unit * query_gain).reshape(rows, heads_here, HEAD), cosine, sine, 1.0
    ).astype(jnp.bfloat16)
    keys = rotate((k_unit * key_gain).reshape(rows, heads_here, HEAD), cosine, sine, 1.0).astype(
        jnp.bfloat16
    )
    block = min(512, rows)
    start = 0
    masked = block_scores(queries, keys, start, length)
    top = jnp.max(masked, axis=-1, keepdims=True)
    expo = jnp.exp(masked - top)
    total = jnp.sum(expo, axis=-1, keepdims=True)
    probs = expo / total
    lse_parts = [top + jnp.log(total)]
    mix_parts = jnp.einsum(
        "hqk,khe->qhe", probs.astype(jnp.bfloat16), values, preferred_element_type=jnp.float32
    )
    attn_mix = mix_parts.reshape(rows, local).astype(jnp.bfloat16)
    attn_branch = lax.psum(matmul(attn_mix, output_weight), "tensor")
    a_scale = lax.rsqrt(jnp.mean(attn_branch * attn_branch, axis=-1, keepdims=True) + EPS)
    a_unit = attn_branch * a_scale
    attn_out = attn_gain * a_unit
    mid = rows_f + attn_out
    mid_low = mid.astype(jnp.bfloat16)
    gate = matmul(mid_low, gate_weight)
    upper = matmul(mid_low, up_weight)
    inner = (jax.nn.silu(gate) * upper).astype(jnp.bfloat16)
    mlp_branch = lax.psum(matmul(inner, down_weight), "tensor")
    m_scale = lax.rsqrt(jnp.mean(mlp_branch * mlp_branch, axis=-1, keepdims=True) + EPS)
    m_unit = mlp_branch * m_scale
    mlp_out = mlp_gain * m_unit
    layer_sum = mid + mlp_out
    mlp_gain_part = jnp.sum(grad_in * m_unit, axis=0)
    d_mlp_branch = post_norm_back(grad_in, m_unit, m_scale, mlp_gain).astype(jnp.bfloat16)
    down_grad = left_inner(inner, d_mlp_branch)
    d_inner = right_inner(d_mlp_branch, down_weight)
    sig = jax.nn.sigmoid(gate)
    d_gate = (d_inner * upper * sig * (1.0 + gate * (1.0 - sig))).astype(jnp.bfloat16)
    d_up = (d_inner * gate * sig).astype(jnp.bfloat16)
    gate_grad = left_inner(mid_low, d_gate)
    up_grad = left_inner(mid_low, d_up)
    d_mid = grad_in + lax.psum(
        right_inner(d_gate, gate_weight) + right_inner(d_up, up_weight), "tensor"
    )
    attn_gain_part = jnp.sum(d_mid * a_unit, axis=0)
    d_attn_branch = post_norm_back(d_mid, a_unit, a_scale, attn_gain).astype(jnp.bfloat16)
    output_grad = left_inner(attn_mix, d_attn_branch)
    d_mix = (
        right_inner(d_attn_branch, output_weight)
        .astype(jnp.bfloat16)
        .reshape(rows, heads_here, HEAD)
    )
    d_query_parts = []
    d_keys = jnp.zeros((rows, heads_here, HEAD), jnp.float32)
    d_values = jnp.zeros((rows, heads_here, HEAD), jnp.float32)
    for number, start in enumerate(range(0, rows, block)):
        masked = block_scores(queries, keys, start, length)
        probs = jnp.exp(masked - lse_parts[number])
        d_probs = jnp.einsum("qhe,khe->hqk", d_mix, values, preferred_element_type=jnp.float32)
        centre = jnp.sum(probs * d_probs, axis=-1, keepdims=True)
        d_scores = (probs * (d_probs - centre)).astype(jnp.bfloat16)
        d_query_parts.append(
            jnp.einsum("hqk,khe->qhe", d_scores, keys, preferred_element_type=jnp.float32)
            / math.sqrt(HEAD)
        )
        d_keys = jnp.einsum(
            "hqk,qhe->khe", d_scores, queries, preferred_element_type=jnp.float32
        ) / math.sqrt(HEAD)
        d_values = jnp.einsum(
            "hqk,qhe->khe", probs.astype(jnp.bfloat16), d_mix, preferred_element_type=jnp.float32
        )
    d_q_hat = rotate(d_query_parts[0], cosine, sine, -1.0).reshape(rows, local)
    d_k_hat = rotate(d_keys, cosine, sine, -1.0).reshape(rows, local)
    query_gain_part = jnp.sum(d_q_hat * q_unit, axis=0)
    key_gain_part = jnp.sum(d_k_hat * k_unit, axis=0)
    q_scaled = d_q_hat * query_gain
    k_scaled = d_k_hat * key_gain
    q_inner, k_inner = lax.psum(
        (jnp.sum(q_scaled * q_unit, axis=-1), jnp.sum(k_scaled * k_unit, axis=-1)), "tensor"
    )
    d_q_raw = (q_scale * (q_scaled - q_unit * (q_inner / D)[:, None])).astype(jnp.bfloat16)
    d_k_raw = (k_scale * (k_scaled - k_unit * (k_inner / D)[:, None])).astype(jnp.bfloat16)
    d_v = d_values.reshape(rows, local).astype(jnp.bfloat16)
    query_grad = left_inner(rows_low, d_q_raw)
    key_grad = left_inner(rows_low, d_k_raw)
    value_grad = left_inner(rows_low, d_v)
    input_terms = (
        right_inner(d_q_raw, query_weight)
        + right_inner(d_k_raw, key_weight)
        + right_inner(d_v, value_weight)
    )
    input_sum = d_mid + lax.psum(input_terms.astype(jnp.bfloat16), "tensor").astype(jnp.float32)
    query_part, key_part, value_part, gate_part, up_part, output_part, down_part = (
        lax.psum_scatter(
            query_grad.astype(jnp.bfloat16), "dp", scatter_dimension=0, tiled=True
        ).astype(jnp.float32),
        lax.psum_scatter(
            key_grad.astype(jnp.bfloat16), "dp", scatter_dimension=0, tiled=True
        ).astype(jnp.float32),
        lax.psum_scatter(
            value_grad.astype(jnp.bfloat16), "dp", scatter_dimension=0, tiled=True
        ).astype(jnp.float32),
        lax.psum_scatter(
            gate_grad.astype(jnp.bfloat16), "dp", scatter_dimension=0, tiled=True
        ).astype(jnp.float32),
        lax.psum_scatter(
            up_grad.astype(jnp.bfloat16), "dp", scatter_dimension=0, tiled=True
        ).astype(jnp.float32),
        lax.psum_scatter(
            output_grad.astype(jnp.bfloat16), "dp", scatter_dimension=1, tiled=True
        ).astype(jnp.float32),
        lax.psum_scatter(
            down_grad.astype(jnp.bfloat16), "dp", scatter_dimension=1, tiled=True
        ).astype(jnp.float32),
    )
    squares = jnp.stack(
        [
            jnp.sum(jnp.where(live, rows_f * rows_f, 0.0)),
            jnp.sum(jnp.where(live, attn_out * attn_out, 0.0)),
            jnp.sum(jnp.where(live, mlp_out * mlp_out, 0.0)),
        ]
    )
    squares, query_gain_grad, key_gain_grad, attn_gain_grad, mlp_gain_grad = lax.psum(
        (squares, query_gain_part, key_gain_part, attn_gain_part, mlp_gain_part), "dp"
    )
    total = jnp.sum(seq_lengths).astype(jnp.float32) * D
    rms_values = jnp.sqrt(squares / total)
    out_low = jnp.where(live, layer_sum, 0.0).astype(jnp.bfloat16).reshape(count, piece, width)
    grad_low = jnp.where(live, input_sum, 0.0).astype(jnp.bfloat16).reshape(count, piece, width)
    out_first, grad_first = return_rows((out_low, grad_low))
    out_second, grad_second = return_rows(
        (jnp.take(out_first, inverse, axis=0), jnp.take(grad_first, inverse, axis=0))
    )
    layer_out = out_second.reshape(1, rows, width)
    input_grad = grad_second.reshape(1, rows, width)
    return (
        layer_out,
        input_grad,
        query_part,
        key_part,
        value_part,
        output_part,
        query_gain_grad,
        key_gain_grad,
        attn_gain_grad,
        gate_part,
        up_part,
        down_part,
        mlp_gain_grad,
        rms_values,
    )


def solution(mesh):
    placed = (
        P("dp", None, None),
        P("dp", None, None),
        P(),
        P(),
        P(None, "tensor"),
        P(None, "tensor"),
        P(None, "tensor"),
        P("tensor", None),
        P("tensor"),
        P("tensor"),
        P(),
        P(None, "tensor"),
        P(None, "tensor"),
        P("tensor", None),
        P(),
    )
    return jax.shard_map(
        body,
        mesh=mesh,
        in_specs=placed,
        out_specs=(
            P("dp", None, None),
            P("dp", None, None),
            P("dp", "tensor"),
            P("dp", "tensor"),
            P("dp", "tensor"),
            P("tensor", "dp"),
            P("tensor"),
            P("tensor"),
            P(),
            P("dp", "tensor"),
            P("dp", "tensor"),
            P("tensor", "dp"),
            P(),
            P(),
        ),
        check_vma=False,
    )
```

profile of v0, /device:TPU:0, one launch (start us, length us, event | category | flops | bytes accessed | tf_op | source)
XLA Modules:
  0.0 1114.2 jit_solution(4149600966942774560)
XLA Ops:
  19.0 8.3 all-reduce.2
  42.5 5.8 all-to-all-start.2
  48.3 46.0 %all-reduce.8.cloned.1.call-done = f32[256,2048]{1,0:T(8,128)} async-done(((f32[256,2048]{1,0:T(8,128)}), f32[256,2048]{1,0:T(8,128)}) %all-reduce.8.cloned.1.call-update) | async-done | bytes 2097168 | tf_op jit(solution)/shard_map/psum | solution.py:142
  97.0 6.3 fusion.52
  104.6 4.2 multiply_convert_fusion.3
  111.8 5.5 all-to-all-start.3
  117.5 7.4 fusion.53
  125.0 52.0 %all-reduce.10.cloned.1.call-done = f32[256,2048]{1,0:T(8,128)} async-done(((f32[256,2048]{1,0:T(8,128)}), f32[256,2048]{1,0:T(8,128)}) %all-reduce.10.cloned.1.call-update) | async-done | bytes 2097168 | tf_op jit(solution)/shard_map/psum | solution.py:151
  178.9 3.5 fusion.14
  183.1 7.2 multiply_convert_fusion.1
  192.7 7.1 convolution_add_fusion.2
  200.1 51.3 %all-reduce.12.cloned.1.call-done = f32[256,2048]{1,0:T(8,128)} async-done(((f32[256,2048]{1,0:T(8,128)}), f32[256,2048]{1,0:T(8,128)}) %all-reduce.12.cloned.1.call-update) | async-done | bytes 2097168 | tf_op jit(solution)/shard_map/psum | solution.py:165
  251.4 5.9 multiply_reduce_fusion
  269.0 5.8 all-reduce.1
  282.1 3.4 convolution_convert_fusion.3
  296.9 7.2 convolution_convert_fusion
  304.1 7.1 convolution_convert_fusion.1
  311.3 7.2 convolution_convert_fusion.2
  318.6 5.8 all-to-all-start
  324.4 3.5 select_convert_fusion
  327.9 36.0 %all-to-all-done = bf16[8,32,2048]{2,1,0:T(8,128)(2,1)} async-done(((bf16[8,32,2048]{2,1,0:T(8,128)(2,1)}), bf16[8,32,2048]{2,1,0:T(8,128)(2,1)}, u32[]{:S(2)}, u32[]{:S(2)}) %all-to-all-start) | async-done | bytes 1048608 | tf_op jit(solution)/shard_map/all_to_all | solution.py:57
  363.9 5.4 all-to-all-start.4
  371.4 23.6 %all-to-all-done.4 = bf16[8,32,2048]{2,1,0:T(8,128)(2,1)} async-done(((bf16[8,32,2048]{2,1,0:T(8,128)(2,1)}), bf16[8,32,2048]{2,1,0:T(8,128)(2,1)}, u32[]{:S(2)}, u32[]{:S(2)}) %all-to-all-start.4) | async-done | bytes 1048608 | tf_op jit(solution)/shard_map/all_to_all | solution.py:58
  400.2 32.7 %all_to_all.30 = bf16[8,32,2048]{2,1,0:T(8,128)(2,1)S(1)} all-to-all(bf16[8,32,2048]{2,1,0:T(8,128)(2,1)S(1)} %get-tuple-element.84), channel_id=1, replica_groups=mesh['dp'=8,'tensor'=4] {'dp'}, dimensions={0} | all-to-all | bytes 2097152 | tf_op jit(solution)/shard_map/all_to_all | solution.py:58
  433.0 4.3 all-to-all-start.1
  439.9 56.8 %all-reduce = (f32[512]{0:T(512)}, f32[512]{0:T(512)}, f32[2048]{0:T(1024)}, f32[2048]{0:T(1024)}, f32[3]{0:T(128)S(1)}) all-reduce(f32[512]{0:T(512)S(1)} %get-tuple-element.51, f32[512]{0:T(512)S(1)} %get-tuple-element.49, f32[2048]{0:T(1024)S(1)} %copy-done.44, ...), channel_id=1, replica_groups=mesh['dp'=8,'tensor'=4] {'dp'}, use_global_device_ids=true, to_apply=%region_27.29 | all-reduce | flops 5123 | bytes 40984 | tf_op jit(solution)/shard_map/psum | solution.py:246
  499.0 3.6 reduce-scatter.10.cloned.1.call-done
  504.5 69.5 %reduce-scatter.8.cloned.1.call-done = bf16[256,512]{0,1:T(8,128)(2,1)} async-done(((bf16[2048,512]{0,1:T(8,128)(2,1)}), bf16[256,512]{0,1:T(8,128)(2,1)}) %reduce-scatter.8.cloned.1.call-update) | async-done | bytes 262160 | tf_op jit(solution)/shard_map/reduce_scatter | solution.py:217
  575.9 69.7 %reduce-scatter.12.cloned.1.call-done = bf16[256,512]{0,1:T(8,128)(2,1)} async-done(((bf16[2048,512]{0,1:T(8,128)(2,1)}), bf16[256,512]{0,1:T(8,128)(2,1)}) %reduce-scatter.12.cloned.1.call-update) | async-done | bytes 262160 | tf_op jit(solution)/shard_map/reduce_scatter | solution.py:223
  647.4 150.1 %reduce-scatter.20.cloned.1.call-done = bf16[2048,256]{1,0:T(8,128)(2,1)} async-done(((bf16[2048,2048]{1,0:T(8,128)(2,1)}), bf16[2048,256]{1,0:T(8,128)(2,1)}) %reduce-scatter.20.cloned.1.call-update) | async-done | bytes 1048592 | tf_op jit(solution)/shard_map/reduce_scatter | solution.py:235
  800.2 149.3 %reduce-scatter.18.cloned.1.call-done = bf16[256,2048]{1,0:T(8,128)(2,1)} async-done(((bf16[2048,2048]{1,0:T(8,128)(2,1)}), bf16[256,2048]{1,0:T(8,128)(2,1)}) %reduce-scatter.18.cloned.1.call-update) | async-done | bytes 1048592 | tf_op jit(solution)/shard_map/reduce_scatter | solution.py:229
  952.3 148.9 %reduce-scatter.16.cloned.1.call-done = bf16[256,2048]{1,0:T(8,128)(2,1)} async-done(((bf16[2048,2048]{1,0:T(8,128)(2,1)}), bf16[256,2048]{1,0:T(8,128)(2,1)}) %reduce-scatter.16.cloned.1.call-update) | async-done | bytes 1048592 | tf_op jit(solution)/shard_map/reduce_scatter | solution.py:226
  (233 shorter events, 97.9 us)
Async XLA Ops:
  7.2 8.7 copy-start
  7.2 87.1 %all-reduce.8.cloned.1.call-start = ((), (), s32[]{:S(2)}) async-start(), calls=%async_computation.13 | async-start | bytes 4194304 | tf_op jit(solution)/shard_map/psum | solution.py:142
  7.3 8.7 copy-start.4
  11.3 246.1 %copy-start.48 = (pred[256]{0:T(512)(128)(4,1)}, pred[256]{0:T(512)(128)(4,1)S(1)}, u32[]{:S(2)}) copy-start(pred[256]{0:T(512)(128)(4,1)S(1)} %iota_compare_fusion.2) | copy-start | bytes 772
  17.5 9.9 copy-start.46
  17.5 13.8 %copy-start.45 = (f32[512]{0:T(512)S(1)}, f32[512]{0:T(512)}, u32[]{:S(2)}) copy-start(f32[512]{0:T(512)} %param.25) | copy-start | bytes 6148
  27.4 7.9 copy-start.50
  27.4 7.9 copy-start.53
  42.5 53.8 %copy-start.43 = (f32[2048]{0:T(1024)S(1)}, f32[2048]{0:T(1024)}, u32[]{:S(2)}) copy-start(f32[2048]{0:T(1024)} %param.27) | copy-start | bytes 24580
  42.5 66.3 %all-to-all-start.2 = ((bf16[8,32,2048]{2,1,0:T(8,128)(2,1)}), bf16[8,32,2048]{2,1,0:T(8,128)(2,1)}, u32[]{:S(2)}, u32[]{:S(2)}) async-start(bf16[8,32,2048]{2,1,0:T(8,128)(2,1)} %bitcast.141), calls=%async_computation.2 | async-start | bytes 2097152 | tf_op jit(solution)/shard_map/all_to_all | solution.py:52
  96.5 8.1 slice-start.2
  96.9 7.7 slice-start.3
  111.8 67.0 %all-to-all-start.3 = ((bf16[8,32,2048]{2,1,0:T(8,128)(2,1)}), bf16[8,32,2048]{2,1,0:T(8,128)(2,1)S(1)}, u32[]{:S(2)}, u32[]{:S(2)}) async-start(bf16[8,32,2048]{2,1,0:T(8,128)(2,1)} %broadcast_select_fusion), calls=%async_computation.3 | async-start | bytes 2097152 | tf_op jit(solution)/shard_map/all_to_all | solution.py:52
  117.3 59.7 %all-reduce.10.cloned.1.call-start = ((), (), s32[]{:S(2)}) async-start(), calls=%async_computation.14 | async-start | bytes 4194304 | tf_op jit(solution)/shard_map/psum | solution.py:151
  124.9 53.9 %copy-start.42 = (f32[2048]{0:T(1024)S(1)}, f32[2048]{0:T(1024)}, u32[]{:S(2)}) copy-start(f32[2048]{0:T(1024)} %param.31) | copy-start | bytes 24580
  124.9 126.5 %all-reduce.12.cloned.1.call-start = ((), (), s32[]{:S(2)}) async-start(), calls=%async_computation.15 | async-start | bytes 4194304 | tf_op jit(solution)/shard_map/psum | solution.py:165
  182.4 7.9 slice-start
  199.8 124.5 %all-reduce.14.cloned.1.call-start = ((), (), s32[]{:S(2)}) async-start(), calls=%async_computation.16 | async-start | bytes 2097152 | tf_op jit(solution)/shard_map/psum | solution.py:215
  267.6 7.3 copy-start.55
  268.7 8.0 copy-start.52
  282.1 215.1 %reduce-scatter.14.cloned.1.call-start = ((), (), s32[]{:S(2)}) async-start(), calls=%async_computation.20 | async-start | bytes 2359296 | tf_op jit(solution)/shard_map/reduce_scatter | solution.py:232
  285.5 217.1 %reduce-scatter.10.cloned.1.call-start = ((), (), s32[]{:S(2)}) async-start(), calls=%async_computation.18 | async-start | bytes 2359296 | tf_op jit(solution)/shard_map/reduce_scatter | solution.py:220
  289.0 285.0 %reduce-scatter.8.cloned.1.call-start = ((), (), s32[]{:S(2)}) async-start(), calls=%async_computation.17 | async-start | bytes 2359296 | tf_op jit(solution)/shard_map/reduce_scatter | solution.py:217
  292.3 353.2 %reduce-scatter.12.cloned.1.call-start = ((), (), s32[]{:S(2)}) async-start(), calls=%async_computation.19 | async-start | bytes 2359296 | tf_op jit(solution)/shard_map/reduce_scatter | solution.py:223
  296.6 501.0 %reduce-scatter.20.cloned.1.call-start = ((), (), s32[]{:S(2)}) async-start(), calls=%async_computation.23 | async-start | bytes 9437184 | tf_op jit(solution)/shard_map/reduce_scatter | solution.py:235
  304.1 645.4 %reduce-scatter.18.cloned.1.call-start = ((), (), s32[]{:S(2)}) async-start(), calls=%async_computation.22 | async-start | bytes 9437184 | tf_op jit(solution)/shard_map/reduce_scatter | solution.py:229
  311.3 789.9 %reduce-scatter.16.cloned.1.call-start = ((), (), s32[]{:S(2)}) async-start(), calls=%async_computation.21 | async-start | bytes 9437184 | tf_op jit(solution)/shard_map/reduce_scatter | solution.py:226
  318.6 45.4 %all-to-all-start = ((bf16[8,32,2048]{2,1,0:T(8,128)(2,1)}), bf16[8,32,2048]{2,1,0:T(8,128)(2,1)}, u32[]{:S(2)}, u32[]{:S(2)}) async-start(bf16[8,32,2048]{2,1,0:T(8,128)(2,1)} %bitcast.134), calls=%async_computation | async-start | bytes 2097152 | tf_op jit(solution)/shard_map/all_to_all | solution.py:57
  327.9 41.5 %copy-start.57 = (s32[8]{0:T(128)S(1)}, s32[8]{0:T(128)}, u32[]{:S(2)}) copy-start(s32[8]{0:T(128)} %param.20) | copy-start | bytes 100
  363.9 31.0 %all-to-all-start.4 = ((bf16[8,32,2048]{2,1,0:T(8,128)(2,1)}), bf16[8,32,2048]{2,1,0:T(8,128)(2,1)}, u32[]{:S(2)}, u32[]{:S(2)}) async-start(bf16[8,32,2048]{2,1,0:T(8,128)(2,1)} %bitcast.136), calls=%async_computation.4 | async-start | bytes 2097152 | tf_op jit(solution)/shard_map/all_to_all | solution.py:58
  400.2 39.7 %copy-start.44 = (f32[2048]{0:T(1024)S(1)}, f32[2048]{0:T(1024)}, u32[]{:S(2)}) copy-start(f32[2048]{0:T(1024)} %get-tuple-element.43) | copy-start | bytes 24580
  433.0 64.2 %all-to-all-start.1 = ((bf16[8,32,2048]{2,1,0:T(8,128)(2,1)}), bf16[8,32,2048]{2,1,0:T(8,128)(2,1)}, u32[]{:S(2)}, u32[]{:S(2)}) async-start(bf16[8,32,2048]{2,1,0:T(8,128)(2,1)} %get-tuple-element.85), calls=%async_computation.1 | async-start | bytes 2097152 | tf_op jit(solution)/shard_map/all_to_all | solution.py:57
  (49 other events, 113.9 us)
Sparse Core Ops, SparseCore 0:
  42.6 51.6 all-reduce.7
  125.1 51.8 all-reduce.9
  200.0 51.4 all-reduce.11
  282.2 36.8 all-reduce.13
  322.4 90.1 reduce-scatter.13
  416.6 85.9 reduce-scatter.9
  506.7 67.1 reduce-scatter.7
  578.1 67.3 reduce-scatter.11
  649.1 148.3 reduce-scatter.19
  801.5 148.0 reduce-scatter.17
  953.1 148.0 reduce-scatter.15
where the time goes:
time: 1120 us; the launch traced here: 1110 us
  waiting for transfers between devices  800 us (71%)
  blocking collectives  104 us (9%)
  matrix products  87.7 us (8%)
  other arithmetic  48.1 us (4%)
  local copies, waits for them, and re-layouts  30.9 us (3%)
  starting transfers between devices  27.9 us (2%)
  between operations  15.9 us (1%)
    reduce_scatter x1, waiting for transfers between devices, body(): lax.psum_scatter(down_grad.astype(jnp.bfloat16), 'dp', scatter_dimension=...  150 us
    reduce_scatter x1, waiting for transfers between devices, body(): lax.psum_scatter(up_grad.astype(jnp.bfloat16), 'dp', scatter_dimension=0,...  149 us
    reduce_scatter x1, waiting for transfers between devices, body(): lax.psum_scatter(gate_grad.astype(jnp.bfloat16), 'dp', scatter_dimension=...  149 us
    reduce_scatter x1, waiting for transfers between devices, body(): lax.psum_scatter(value_grad.astype(jnp.bfloat16), 'dp', scatter_dimension...  69.7 us
    reduce_scatter x1, waiting for transfers between devices, body(): lax.psum_scatter(query_grad.astype(jnp.bfloat16), 'dp', scatter_dimension...  69.5 us
    psum x1, blocking collectives, body(): lax.psum((squares, query_gain_part, key_gain_part, attn_gain_part, mlp_ga...  56.8 us
    psum x1, waiting for transfers between devices, body(): mlp_branch = lax.psum(matmul(inner, down_weight), 'tensor')  52 us
    psum x1, waiting for transfers between devices, body(): lax.psum(right_inner(d_gate, gate_weight) + right_inner(d_up, up_weight),...  51.3 us
  transfers between devices with their start and end apart: 16, of which 11 were waited for; matrix products, arithmetic and copies ran while one was open for 7% of the time, Pallas kernels for 0%

commit v1 on v0

v1 whole, which is shorter than its diff:
```python
import math

import jax
import jax.numpy as jnp
from jax import lax
from jax.sharding import PartitionSpec as P

D = 2048
HEAD = 128
EPS = 1e-06
F32 = jnp.float32
BF16 = jnp.bfloat16


def matmul(left, right):
    return jnp.dot(left, right, preferred_element_type=F32)


def left_inner(left, right):
    return lax.dot_general(left, right, (((0,), (0,)), ((), ())), preferred_element_type=F32)


def right_inner(left, right):
    return lax.dot_general(left, right, (((1,), (1,)), ((), ())), preferred_element_type=F32)


def rope_tables(rows, width):
    places = jnp.arange(rows, dtype=F32)
    freq = jnp.power(F32(500000.0), -jnp.arange(width // 2, dtype=F32) * (2.0 / width))
    angle = places[:, None] * freq[None, :]
    return (jnp.cos(angle), jnp.sin(angle))


def rotate(field, cosine, sine, sign):
    half = field.shape[-1] // 2
    first = field[..., :half]
    second = field[..., half:]
    cosine = cosine[:, None, :]
    sine = sine[:, None, :] * sign
    return jnp.concatenate(
        [first * cosine - second * sine, second * cosine + first * sine], axis=-1
    )


class Grid:
    def __init__(self, count):
        self.count = count
        self.lanes = 2 ** ((count.bit_length() - 1) // 2)
        self.groups = count // self.lanes
        me = lax.axis_index("dp")
        self.group = me // self.lanes
        self.lane = me % self.lanes

    def shift_groups(self, field, step):
        pairs = [
            (g * self.lanes + a, ((g + step) % self.groups) * self.lanes + a)
            for g in range(self.groups)
            for a in range(self.lanes)
        ]
        return lax.ppermute(field, "dp", pairs)

    def shift_lanes(self, field, step):
        pairs = [
            (g * self.lanes + a, g * self.lanes + (a + step) % self.lanes)
            for g in range(self.groups)
            for a in range(self.lanes)
        ]
        return lax.ppermute(field, "dp", pairs)

    def ring(self, field):
        found = []
        for _ in range(self.groups - 1):
            field = self.shift_groups(field, 1)
            found.append(field)
        return found

    def total(self, field):
        step = 1
        while step < self.count:
            field = field + lax.ppermute(
                field, "dp", [(i, i ^ step) for i in range(self.count)]
            )
            step *= 2
        return field


def sibling(field):
    size = lax.axis_size("tensor")
    return lax.ppermute(field, "tensor", [(i, i ^ 1) for i in range(size)])


def across(field):
    size = lax.axis_size("tensor")
    return lax.ppermute(field, "tensor", [(i, (i + 2) % size) for i in range(size)])


def reduce_rows(partial):
    return lax.psum_scatter(partial, "tensor", scatter_dimension=0, tiled=True)


def gather_rows(shard):
    return lax.all_gather(shard, "tensor", axis=0, tiled=True)


def shared_ring(grid, rows_low):
    core = lax.axis_index("tensor") % 2
    half = rows_low.shape[0] // 2
    mine = lax.dynamic_slice_in_dim(rows_low, core * half, half, axis=0)
    pieces = []
    for piece in grid.ring(mine):
        pieces += [piece, sibling(piece)]
    return jnp.concatenate(pieces, axis=0)


def body(
    hidden_in,
    upstream_grad,
    seq_lengths,
    position_order,
    query_weight,
    key_weight,
    value_weight,
    output_weight,
    query_gain,
    key_gain,
    attn_gain,
    gate_weight,
    up_weight,
    down_weight,
    mlp_gain,
):
    count = lax.axis_size("dp")
    ways = lax.axis_size("tensor")
    myself = lax.axis_index("dp")
    part = lax.axis_index("tensor")
    grid = Grid(count)
    index = jnp.arange(count, dtype=jnp.int32)
    inverse = jnp.sum(
        index[None, :] * (position_order[None, :] == index[:, None]).astype(jnp.int32), axis=1
    )
    rows = hidden_in.shape[1]
    width = hidden_in.shape[2]
    shard = rows // ways
    piece = shard // count
    seq_here = jnp.sum(jnp.where(index == myself, position_order, 0))
    length = jnp.sum(jnp.where(index == seq_here, seq_lengths, 0))
    live = (part * shard + jnp.arange(shard, dtype=jnp.int32) < length)[:, None]

    def exchange(pieces):
        return lax.all_to_all(pieces, "dp", split_axis=0, concat_axis=0, tiled=True)

    def my_rows(field):
        return lax.dynamic_slice_in_dim(field, part * shard, shard, axis=0)

    first = exchange(my_rows(upstream_grad[0]).reshape(count, piece, width))
    second = exchange(jnp.take(first, position_order, axis=0))
    grad_in = jnp.where(live, second.reshape(shard, width).astype(F32), 0.0)

    rows_low = hidden_in[0]
    my_low = my_rows(rows_low)
    rows_f = my_low.astype(F32)
    local = query_weight.shape[1]
    heads_here = local // HEAD
    strip = width // grid.groups
    tile = width // count

    def strip_of(field, group):
        return lax.dynamic_slice_in_dim(field, group * strip, strip, axis=1)

    def strips(field):
        found = [strip_of(field, grid.group)]
        for step in range(1, grid.groups):
            found.append(
                grid.shift_groups(
                    strip_of(field, (grid.group + step) % grid.groups), step
                )
            )
        return jnp.concatenate(found, axis=0)

    def tile_of(field, lane):
        return lax.dynamic_slice_in_dim(field, lane * tile, tile, axis=1)

    def reduced(product, field):
        sent = []
        for step in range(1, grid.lanes):
            other = product(tile_of(field, (grid.lane + step) % grid.lanes)).astype(BF16)
            sent.append(grid.shift_lanes(other, step))
        mine = product(tile_of(field, grid.lane))
        for other in sent:
            mine = mine + other.astype(F32)
        return mine

    hidden_strips = strips(rows_low)

    q_raw = matmul(rows_low, query_weight)
    k_raw = matmul(rows_low, key_weight)
    values = matmul(rows_low, value_weight).astype(BF16).reshape(rows, heads_here, HEAD)
    q_total, k_total = lax.psum(
        (jnp.sum(q_raw * q_raw, axis=-1), jnp.sum(k_raw * k_raw, axis=-1)), "tensor"
    )
    q_scale = lax.rsqrt(q_total / D + EPS)[:, None]
    k_scale = lax.rsqrt(k_total / D + EPS)[:, None]
    q_unit = q_raw * q_scale
    k_unit = k_raw * k_scale
    cosine, sine = rope_tables(rows, HEAD)
    queries = rotate(
        (q_unit * query_gain).reshape(rows, heads_here, HEAD), cosine, sine, 1.0
    ).astype(BF16)
    keys = rotate((k_unit * key_gain).reshape(rows, heads_here, HEAD), cosine, sine, 1.0).astype(
        BF16
    )
    ids = jnp.arange(rows, dtype=jnp.int32)
    allowed = (ids[None, :] <= ids[:, None]) & (ids[None, :] < length)
    scores = jnp.einsum("qhe,khe->hqk", queries, keys, preferred_element_type=F32) / math.sqrt(HEAD)
    masked = jnp.where(allowed[None], scores, -1e30)
    top = jnp.max(masked, axis=-1, keepdims=True)
    expo = jnp.exp(masked - top)
    probs = expo / jnp.sum(expo, axis=-1, keepdims=True)
    probs_low = probs.astype(BF16)
    mix = jnp.einsum("hqk,khe->qhe", probs_low, values, preferred_element_type=F32)
    attn_mix = mix.reshape(rows, local).astype(BF16)
    mix_all = jnp.concatenate([attn_mix] + grid.ring(attn_mix), axis=0)

    branch = reduce_rows(matmul(attn_mix, output_weight))
    a_scale = lax.rsqrt(jnp.mean(branch * branch, axis=-1, keepdims=True) + EPS)
    a_unit = branch * a_scale
    attn_out = attn_gain * a_unit
    mid = rows_f + attn_out
    mid_low = gather_rows(mid.astype(BF16))
    mid_others = shared_ring(grid, mid_low)

    gate = matmul(mid_low, gate_weight)
    upper = matmul(mid_low, up_weight)
    sig = jax.nn.sigmoid(gate)
    inner = (gate * sig * upper).astype(BF16)
    m_branch = reduce_rows(matmul(inner, down_weight))
    m_scale = lax.rsqrt(jnp.mean(m_branch * m_branch, axis=-1, keepdims=True) + EPS)
    m_unit = m_branch * m_scale
    mlp_out = mlp_gain * m_unit
    layer_sum = mid + mlp_out
    mlp_gain_part = jnp.sum(grad_in * m_unit, axis=0)
    g_m = grad_in * mlp_gain
    d_mlp_mine = (
        m_scale * (g_m - m_unit * jnp.mean(g_m * m_unit, axis=-1, keepdims=True))
    ).astype(BF16)
    d_mlp = gather_rows(d_mlp_mine)
    d_mlp_others = shared_ring(grid, d_mlp)

    def inner_back(gate, upper, d_mlp):
        d_inner = right_inner(d_mlp, down_weight)
        sig = jax.nn.sigmoid(gate)
        d_gate = (d_inner * upper * sig * (1.0 + gate * (1.0 - sig))).astype(BF16)
        d_up = (d_inner * gate * sig).astype(BF16)
        return d_gate, d_up

    d_gate, d_up = inner_back(gate, upper, d_mlp)
    d_mid = grad_in + reduce_rows(
        right_inner(d_gate, gate_weight) + right_inner(d_up, up_weight)
    )
    attn_gain_part = jnp.sum(d_mid * a_unit, axis=0)
    g_a = d_mid * attn_gain
    d_branch = gather_rows(
        (a_scale * (g_a - a_unit * jnp.mean(g_a * a_unit, axis=-1, keepdims=True))).astype(BF16)
    )
    d_branch_strips = strips(d_branch)
    d_mix = right_inner(d_branch, output_weight).astype(BF16).reshape(rows, heads_here, HEAD)
    d_probs = jnp.einsum("qhe,khe->hqk", d_mix, values, preferred_element_type=F32)
    centre = jnp.sum(probs * d_probs, axis=-1, keepdims=True)
    d_scores = (probs * (d_probs - centre)).astype(BF16)
    d_queries = jnp.einsum("hqk,khe->qhe", d_scores, keys, preferred_element_type=F32) / math.sqrt(HEAD)
    d_keys = jnp.einsum("hqk,qhe->khe", d_scores, queries, preferred_element_type=F32) / math.sqrt(HEAD)
    d_values = jnp.einsum("hqk,qhe->khe", probs_low, d_mix, preferred_element_type=F32)
    d_q_hat = rotate(d_queries, cosine, sine, -1.0).reshape(rows, local)
    d_k_hat = rotate(d_keys, cosine, sine, -1.0).reshape(rows, local)
    query_gain_part = jnp.sum(d_q_hat * q_unit, axis=0)
    key_gain_part = jnp.sum(d_k_hat * k_unit, axis=0)
    q_scaled = d_q_hat * query_gain
    k_scaled = d_k_hat * key_gain
    q_inner, k_inner = lax.psum(
        (jnp.sum(q_scaled * q_unit, axis=-1), jnp.sum(k_scaled * k_unit, axis=-1)), "tensor"
    )
    d_q_raw = (q_scale * (q_scaled - q_unit * (q_inner / D)[:, None])).astype(BF16)
    d_k_raw = (k_scale * (k_scaled - k_unit * (k_inner / D)[:, None])).astype(BF16)
    d_v = d_values.reshape(rows, local).astype(BF16)
    d_heads = jnp.concatenate([d_q_raw, d_k_raw, d_v], axis=1)
    d_heads_all = jnp.concatenate([d_heads] + grid.ring(d_heads), axis=0)

    input_sum = d_mid + reduce_rows(
        right_inner(d_q_raw, query_weight)
        + right_inner(d_k_raw, key_weight)
        + right_inner(d_v, value_weight)
    )

    gate_o = matmul(mid_others, gate_weight)
    upper_o = matmul(mid_others, up_weight)
    inner_o = (jax.nn.silu(gate_o) * upper_o).astype(BF16)
    d_gate_o, d_up_o = inner_back(gate_o, upper_o, d_mlp_others)

    def strip_all(own, others):
        return jnp.concatenate([strip_of(own, grid.group), strip_of(others, grid.group)], axis=0)

    mid_strips = strip_all(mid_low, mid_others)
    d_mlp_strips = strip_all(d_mlp, d_mlp_others)
    d_gate_all = jnp.concatenate([d_gate, d_gate_o], axis=0)
    d_up_all = jnp.concatenate([d_up, d_up_o], axis=0)
    inner_all = jnp.concatenate([inner, inner_o], axis=0)
    gate_part = reduced(lambda tile: left_inner(tile, d_gate_all), mid_strips)
    up_part = reduced(lambda tile: left_inner(tile, d_up_all), mid_strips)
    down_part = reduced(lambda tile: left_inner(inner_all, tile), d_mlp_strips)
    output_part = reduced(lambda tile: left_inner(mix_all, tile), d_branch_strips)
    heads_part = reduced(lambda tile: left_inner(tile, d_heads_all), hidden_strips)
    query_part = heads_part[:, :local]
    key_part = heads_part[:, local : 2 * local]
    value_part = heads_part[:, 2 * local :]

    squares = jnp.stack(
        [
            jnp.sum(jnp.where(live, rows_f * rows_f, 0.0)),
            jnp.sum(jnp.where(live, attn_out * attn_out, 0.0)),
            jnp.sum(jnp.where(live, mlp_out * mlp_out, 0.0)),
        ]
    )
    shared = jnp.concatenate([attn_gain_part, mlp_gain_part, squares])
    shared = shared + sibling(shared)
    shared = shared + across(shared)
    sums = grid.total(jnp.concatenate([shared, query_gain_part, key_gain_part]))
    attn_gain_grad = sums[:width]
    mlp_gain_grad = sums[width : 2 * width]
    squares = sums[2 * width : 2 * width + 3]
    query_gain_grad = sums[2 * width + 3 : 2 * width + 3 + local]
    key_gain_grad = sums[2 * width + 3 + local :]
    rms_values = jnp.sqrt(squares / (jnp.sum(seq_lengths).astype(F32) * D))

    def give_back(field):
        pieces = exchange(jnp.where(live, field, 0.0).astype(BF16).reshape(count, piece, width))
        pieces = exchange(jnp.take(pieces, inverse, axis=0))
        return gather_rows(pieces.reshape(shard, width))[None]

    return (
        give_back(layer_sum),
        give_back(input_sum),
        query_part,
        key_part,
        value_part,
        output_part,
        query_gain_grad,
        key_gain_grad,
        attn_gain_grad,
        gate_part,
        up_part,
        down_part,
        mlp_gain_grad,
        rms_values,
    )


def solution(mesh):
    placed = (
        P("dp", None, None),
        P("dp", None, None),
        P(),
        P(),
        P(None, "tensor"),
        P(None, "tensor"),
        P(None, "tensor"),
        P("tensor", None),
        P("tensor"),
        P("tensor"),
        P(),
        P(None, "tensor"),
        P(None, "tensor"),
        P("tensor", None),
        P(),
    )
    return jax.shard_map(
        body,
        mesh=mesh,
        in_specs=placed,
        out_specs=(
            P("dp", None, None),
            P("dp", None, None),
            P("dp", "tensor"),
            P("dp", "tensor"),
            P("dp", "tensor"),
            P("tensor", "dp"),
            P("tensor"),
            P("tensor"),
            P(),
            P("dp", "tensor"),
            P("dp", "tensor"),
            P("tensor", "dp"),
            P(),
            P(),
        ),
        check_vma=False,
    )
```

time: 1120 us -> 537 us (0.48)
  waiting for transfers between devices: 800 us -> 219 us
  blocking collectives: 104 us -> 14.3 us
  matrix products: 87.7 us -> 136 us
  starting transfers between devices: 27.9 us -> 60.3 us
  local copies, waits for them, and re-layouts: 30.9 us -> 44 us
    reduce_scatter x7 -> x4, waiting for transfers between devices: 591 us -> 38.9 us  [reduce_rows(): return lax.psum_scatter(partial, 'tensor', scatter_dimension=0, tiled=True)]
    psum x4 -> x0, waiting for transfers between devices: 149 us -> none  [the longest x1 52 us: body(): mlp_branch = lax.psum(matmul(inner, down_weight), 'tensor')]
    ppermute x0 -> x34, waiting for transfers between devices: none -> 109 us  [the longest x18 64 us: shift_groups(): return lax.ppermute(field, 'dp', pairs)]
    psum x1 -> x0, blocking collectives: 56.8 us -> none  [body(): lax.psum((squares, query_gain_part, key_gain_part, attn_gain_part, mlp_ga...]
    all_to_all x1 -> x0, blocking collectives: 32.7 us -> none  [return_rows(): lax.all_to_all(pieces[1], 'dp', split_axis=0, concat_axis=0, tiled=True)]
    ppermute x0 -> x34, starting transfers between devices: none -> 31.2 us  [the longest x18 21.2 us: shift_groups(): return lax.ppermute(field, 'dp', pairs)]
    dot_general x13 -> x14, matrix products: 31.6 us -> 60.1 us  [the longest x9 52.5 us: matmul(): return jnp.dot(left, right, preferred_element_type=F32)]
    all_gather x0 -> x5, waiting for transfers between devices: none -> 19 us  [gather_rows(): return lax.all_gather(shard, 'tensor', axis=0, tiled=True)]
  transfers between devices with their start and end apart: 16 -> 49, of which waited for: 11 -> 18; matrix products, arithmetic and copies ran while one was open for 7% -> 29% of each run, Pallas kernels for 0% -> 0%
where the time goes in v1:
time: 537 us; the launch traced here: 530 us
  waiting for transfers between devices  219 us (41%)
  matrix products  136 us (25%)
  starting transfers between devices  60.3 us (11%)
  local copies, waits for them, and re-layouts  44 us (8%)
  other arithmetic  40.4 us (8%)
  between operations  16 us (3%)
  blocking collectives  14.3 us (3%)
    ppermute x18, waiting for transfers between devices, shift_groups(): return lax.ppermute(field, 'dp', pairs)  64 us
    dot_general x9, matrix products, matmul(): return jnp.dot(left, right, preferred_element_type=F32)  52.5 us
    all_to_all x6, waiting for transfers between devices, exchange(): return lax.all_to_all(pieces, 'dp', split_axis=0, concat_axis=0, tiled=True)  52.1 us
    reduce_scatter x4, waiting for transfers between devices, reduce_rows(): return lax.psum_scatter(partial, 'tensor', scatter_dimension=0, tiled=True)  38.9 us
    dot_general x8, matrix products, right_inner(): lax.dot_general(left, right, (((1,), (1,)), ((), ())), preferred_element_...  38.6 us
    dot_general x10, matrix products, left_inner(): lax.dot_general(left, right, (((0,), (0,)), ((), ())), preferred_element_...  36.2 us
    all_to_all x6, starting transfers between devices, exchange(): return lax.all_to_all(pieces, 'dp', split_axis=0, concat_axis=0, tiled=True)  28.3 us
    ppermute x3, waiting for transfers between devices, total(): lax.ppermute(field, 'dp', [(i, i ^ step) for i in range(self.count)])  27 us
  transfers between devices with their start and end apart: 49, of which 18 were waited for; matrix products, arithmetic and copies ran while one was open for 29% of the time, Pallas kernels for 0%

profile of v1, /device:TPU:0, one launch (start us, length us, event | category | flops | bytes accessed | tf_op | source)
XLA Modules:
  0.0 530.1 jit_solution(5308054024246077389)
XLA Ops:
  18.8 8.4 %all-reduce.1 = (f32[256]{0:T(256)S(1)}, f32[256]{0:T(256)S(1)}) all-reduce(f32[256]{0:T(256)S(1)} %get-tuple-element.76, f32[256]{0:T(256)S(1)} %get-tuple-element.78), channel_id=1, replica_groups=mesh['dp'=8,'tensor'=4] {'tensor'}, use_global_device_ids=true, to_apply=%region_5.6 | all-reduce | flops 512 | bytes 4096 | tf_op jit(solution)/shard_map/psum | solution.py:198
  45.5 31.8 %reduce-scatter.5.cloned.1.call-done = f32[64,2048]{1,0:T(8,128)} async-done(((f32[256,2048]{1,0:T(8,128)}), f32[64,2048]{1,0:T(8,128)}) %reduce-scatter.5.cloned.1.call-update) | async-done | bytes 524304 | tf_op jit(solution)/shard_map/reduce_scatter | solution.py:98
  80.8 16.5 %all-gather.6.cloned.1.call-done = bf16[256,2048]{1,0:T(8,128)(2,1)} async-done(((bf16[64,2048]{1,0:T(8,128)(2,1)}), bf16[256,2048]{1,0:T(8,128)(2,1)}) %all-gather.6.cloned.1.call-update) | async-done | bytes 1048592 | tf_op jit(solution)/shard_map/all_gather | solution.py:102
  97.3 6.2 %fusion.91 = f32[256,2048]{1,0:T(8,128)S(1)} fusion(bf16[256,2048]{1,0:T(8,128)(2,1)} %all-gather.6.cloned.1.call-done, bf16[2048,2048]{1,0:T(8,128)(2,1)} %param.28), kind=kOutput, calls=%fused_computation.221 | convolution fusion | flops 2147483648 | bytes 11534336 | tf_op jit(solution)/shard_map/dot_general | solution.py:16
  103.5 8.0 %multiply_convert_fusion.5 = (bf16[256,2048]{1,0:T(8,128)(2,1)S(1)}, f32[256,2048]{1,0:T(8,128)}) fusion(f32[256,2048]{1,0:T(8,128)S(1)} %fusion.91, bf16[256,2048]{1,0:T(8,128)(2,1)S(1)} %copy-done.38, bf16[2048,2048]{1,0:T(8,128)(2,1)} %param.29), kind=kOutput, calls=%fused_computation.31 | convolution fusion | flops 2150629376 | bytes 14680064 | tf_op jit(solution)/shard_map/dot_general | solution.py:16
  117.9 5.5 %all-to-all-start.2 = ((bf16[8,8,2048]{2,1,0:T(8,128)(2,1)}), bf16[8,8,2048]{2,1,0:T(8,128)(2,1)}, u32[]{:S(2)}, u32[]{:S(2)}) async-start(bf16[8,8,2048]{2,1,0:T(8,128)(2,1)} %dynamic-slice_bitcast_fusion.4), calls=%async_computation.4 | async-start | bytes 524288 | tf_op jit(solution)/shard_map/all_to_all | solution.py:150
  124.5 8.3 %all-to-all-done.2 = bf16[8,8,2048]{2,1,0:T(8,128)(2,1)} async-done(((bf16[8,8,2048]{2,1,0:T(8,128)(2,1)}), bf16[8,8,2048]{2,1,0:T(8,128)(2,1)}, u32[]{:S(2)}, u32[]{:S(2)}) %all-to-all-start.2) | async-done | bytes 262176 | tf_op jit(solution)/shard_map/all_to_all | solution.py:150
  140.7 7.0 %reduce-scatter.7.cloned.1.call-done = f32[64,2048]{1,0:T(8,128)} async-done(((f32[256,2048]{1,0:T(8,128)}), f32[64,2048]{1,0:T(8,128)}) %reduce-scatter.7.cloned.1.call-update) | async-done | bytes 524304 | tf_op jit(solution)/shard_map/reduce_scatter | solution.py:98
  164.7 7.9 %collective-permute-done.19 = bf16[128,2048]{1,0:T(8,128)(2,1)} collective-permute-done((bf16[128,2048]{1,0:T(8,128)(2,1)}, bf16[128,2048]{1,0:T(8,128)(2,1)}, u32[]{:S(2)}, u32[]{:S(2)}) %collective-permute-start.19) | collective-permute-done | bytes 524320 | tf_op jit(solution)/shard_map/ppermute | solution.py:60
  173.2 7.8 %multiply_convert_fusion.3 = (bf16[256,2048]{1,0:T(8,128)(2,1)S(1)}, bf16[256,2048]{1,0:T(8,128)(2,1)S(1)}) fusion(f32[256,2048]{1,0:T(8,128)} %copy-done.74, f32[256,2048]{1,0:T(8,128)} %get-tuple-element.83, bf16[256,2048]{1,0:T(8,128)(2,1)} %all-gather.10.cloned.1.call-done, bf16[2048,2048]{1,0:T(8,128)(2,1)} %param.30), kind=kOutput, calls=%fused_computation.29 | convolution fusion | flops 2154299392 | bytes 15728640 | tf_op jit(solution)/shard_map/dot_general | solution.py:24
  181.0 6.5 %fusion.93 = f32[256,2048]{1,0:T(8,128)S(1)} fusion(bf16[256,2048]{1,0:T(8,128)(2,1)S(1)} %get-tuple-element.36, bf16[2048,2048]{1,0:T(8,128)(2,1)} %param.28), kind=kOutput, calls=%fused_computation.223 | convolution fusion | flops 2147483648 | bytes 11534336 | tf_op jit(solution)/shard_map/dot_general | solution.py:24
  187.5 7.1 %convolution_add_fusion.3 = f32[256,2048]{1,0:T(8,128)} fusion(f32[256,2048]{1,0:T(8,128)S(1)} %fusion.93, bf16[256,2048]{1,0:T(8,128)(2,1)S(1)} %get-tuple-element.35, bf16[2048,2048]{1,0:T(8,128)(2,1)} %param.29), kind=kOutput, calls=%fused_computation.21 | convolution fusion | flops 2148007936 | bytes 13631488 | tf_op jit(solution)/shard_map/dot_general | solution.py:24
  197.7 18.6 %collective-permute-done.1 = bf16[256,512]{1,0:T(8,128)(2,1)} collective-permute-done((bf16[256,512]{1,0:T(8,128)(2,1)}, bf16[256,512]{1,0:T(8,128)(2,1)}, u32[]{:S(2)}, u32[]{:S(2)}) %collective-permute-start.1) | collective-permute-done | bytes 262176 | tf_op jit(solution)/shard_map/ppermute | solution.py:60
  222.3 13.3 %collective-permute-done.23 = bf16[128,2048]{1,0:T(8,128)(2,1)S(1)} collective-permute-done((bf16[128,2048]{1,0:T(8,128)(2,1)S(1)}, bf16[128,2048]{1,0:T(8,128)(2,1)S(1)}, u32[]{:S(2)}, u32[]{:S(2)}) %collective-permute-start.23) | collective-permute-done | bytes 524320 | tf_op jit(solution)/shard_map/ppermute | solution.py:60
  237.6 14.4 %collective-permute-done.25 = bf16[128,2048]{1,0:T(8,128)(2,1)} collective-permute-done((bf16[128,2048]{1,0:T(8,128)(2,1)S(1)}, bf16[128,2048]{1,0:T(8,128)(2,1)}, u32[]{:S(2)}, u32[]{:S(2)}) %collective-permute-start.25) | collective-permute-done | bytes 524320 | tf_op jit(solution)/shard_map/ppermute | solution.py:60
  252.0 10.7 %fusion.96 = f32[768,2048]{1,0:T(8,128)} fusion(bf16[768,2048]{1,0:T(8,128)(2,1)S(1)} %constant_dynamic-update-slice_fusion, bf16[2048,2048]{1,0:T(8,128)(2,1)} %param.28), kind=kOutput, calls=%fused_computation.226 | convolution fusion | flops 6442450944 | bytes 17825792 | tf_op jit(solution)/shard_map/dot_general | solution.py:16
  263.7 4.0 collective-permute-done.27
  276.7 5.8 %collective-permute-done.29 = bf16[128,2048]{1,0:T(8,128)(2,1)} collective-permute-done((bf16[128,2048]{1,0:T(8,128)(2,1)}, bf16[128,2048]{1,0:T(8,128)(2,1)}, u32[]{:S(2)}, u32[]{:S(2)}) %collective-permute-start.29) | collective-permute-done | bytes 524320 | tf_op jit(solution)/shard_map/ppermute | solution.py:60
  302.6 5.9 %all-reduce = (f32[256]{0:T(256)S(1)}, f32[256]{0:T(256)S(1)}) all-reduce(f32[256]{0:T(256)S(1)} %get-tuple-element.20, f32[256]{0:T(256)S(1)} %get-tuple-element.18), channel_id=1, replica_groups=mesh['dp'=8,'tensor'=4] {'tensor'}, use_global_device_ids=true, to_apply=%region_18.20 | all-reduce | flops 512 | bytes 4096 | tf_op jit(solution)/shard_map/psum | solution.py:279
  316.2 10.2 %fusion.95 = f32[768,2048]{1,0:T(8,128)S(1)} fusion(bf16[768,2048]{1,0:T(8,128)(2,1)} %copy-done.41, bf16[2048,2048]{1,0:T(8,128)(2,1)} %param.30), kind=kOutput, calls=%fused_computation.225 | convolution fusion | flops 6442450944 | bytes 17825792 | tf_op jit(solution)/shard_map/dot_general | solution.py:24
  326.5 15.1 %multiply_convert_fusion = (bf16[768,2048]{1,0:T(8,128)(2,1)S(1)}, bf16[768,2048]{1,0:T(8,128)(2,1)}, bf16[768,2048]{1,0:T(8,128)(2,1)}) fusion(f32[768,2048]{1,0:T(8,128)} %fusion.96, f32[768,2048]{1,0:T(8,128)S(1)} %fusion.95, bf16[768,2048]{1,0:T(8,128)(2,1)S(1)} %copy-done.40, bf16[2048,2048]{1,0:T(8,128)(2,1)} %param.29), kind=kOutput, calls=%fused_computation.4 | convolution fusion | flops 6467616768 | bytes 33554432 | tf_op jit(solution)/shard_map/dot_general | solution.py:16
  345.7 4.6 all-to-all-start
  355.4 20.3 %all-to-all-done = bf16[8,8,2048]{2,1,0:T(8,128)(2,1)S(1)} async-done(((bf16[8,8,2048]{2,1,0:T(8,128)(2,1)}), bf16[8,8,2048]{2,1,0:T(8,128)(2,1)S(1)}, u32[]{:S(2)}, u32[]{:S(2)}) %all-to-all-start) | async-done | bytes 262176 | tf_op jit(solution)/shard_map/all_to_all | solution.py:150
  379.4 4.4 fusion.8
  387.7 4.5 fusion.7
  394.6 6.0 %all-to-all-start.5 = ((bf16[8,8,2048]{2,1,0:T(8,128)(2,1)}), bf16[8,8,2048]{2,1,0:T(8,128)(2,1)S(1)}, u32[]{:S(2)}, u32[]{:S(2)}) async-start(bf16[8,8,2048]{2,1,0:T(8,128)(2,1)} %get-tuple-element.69), calls=%async_computation.9 | async-start | bytes 524288 | tf_op jit(solution)/shard_map/all_to_all | solution.py:150
  403.6 5.3 convert_add_fusion
  410.4 22.4 %all-to-all-done.5 = bf16[8,8,2048]{2,1,0:T(8,128)(2,1)S(1)} async-done(((bf16[8,8,2048]{2,1,0:T(8,128)(2,1)}), bf16[8,8,2048]{2,1,0:T(8,128)(2,1)S(1)}, u32[]{:S(2)}, u32[]{:S(2)}) %all-to-all-start.5) | async-done | bytes 262176 | tf_op jit(solution)/shard_map/all_to_all | solution.py:150
  433.6 5.2 convert_add_fusion.1
  453.4 26.8 %collective-permute-done.18 = f32[5123]{0:T(1024)S(1)} collective-permute-done((f32[5123]{0:T(1024)S(1)}, f32[5123]{0:T(1024)S(1)}, u32[]{:S(2)}, u32[]{:S(2)}) %collective-permute-start.18) | collective-permute-done | bytes 20524 | tf_op jit(solution)/shard_map/ppermute | solution.py:80
  481.0 5.1 all-to-all-start.1
  496.3 15.8 %collective-permute-done.13 = bf16[512,256]{1,0:T(8,128)(2,1)S(1)} collective-permute-done((bf16[512,256]{1,0:T(8,128)(2,1)S(1)}, bf16[512,256]{1,0:T(8,128)(2,1)S(1)}, u32[]{:S(2)}, u32[]{:S(2)}) %collective-permute-start.13) | collective-permute-done | bytes 262176 | tf_op jit(solution)/shard_map/ppermute | solution.py:68
  (354 shorter events, 174.6 us)
Async XLA Ops:
  7.2 70.1 %reduce-scatter.5.cloned.1.call-start = ((), (), s32[]{:S(2)}) async-start(), calls=%async_computation.10 | async-start | bytes 2621440 | tf_op jit(solution)/shard_map/reduce_scatter | solution.py:98
  45.4 51.9 %all-gather.6.cloned.1.call-start = ((), (), s32[]{:S(2)}) async-start(), calls=%async_computation.11 | async-start | bytes 1310720 | tf_op jit(solution)/shard_map/all_gather | solution.py:102
  80.4 67.3 %reduce-scatter.7.cloned.1.call-start = ((), (), s32[]{:S(2)}) async-start(), calls=%async_computation.12 | async-start | bytes 2621440 | tf_op jit(solution)/shard_map/reduce_scatter | solution.py:98
  139.5 33.6 %all-gather.10.cloned.1.call-start = ((), (), s32[]{:S(2)}) async-start(), calls=%async_computation.14 | async-start | bytes 1310720 | tf_op jit(solution)/shard_map/all_gather | solution.py:102
  153.6 114.1 %reduce-scatter.9.cloned.1.call-start = ((), (), s32[]{:S(2)}) async-start(), calls=%async_computation.15 | async-start | bytes 2621440 | tf_op jit(solution)/shard_map/reduce_scatter | solution.py:98
  157.0 39.6 %collective-permute-start.7 = (bf16[256,512]{0,1:T(8,128)(2,1)}, bf16[256,512]{0,1:T(8,128)(2,1)}, u32[]{:S(2)}, u32[]{:S(2)}) collective-permute-start(bf16[256,512]{0,1:T(8,128)(2,1)} %bitcast.139), channel_id=1, source_target_pairs={{0,8},{4,12},{8,16},{12,20},{16,24},{20,28},{24,0},{28,4},{1,9},{5... | collective-permute-start | bytes 786440 | tf_op jit(solution)/shard_map/ppermute | solution.py:60
  159.5 35.9 %collective-permute-start = (bf16[256,512]{1,0:T(8,128)(2,1)}, bf16[256,512]{1,0:T(8,128)(2,1)S(1)}, u32[]{:S(2)}, u32[]{:S(2)}) collective-permute-start(bf16[256,512]{1,0:T(8,128)(2,1)} %get-tuple-element.50), channel_id=1, source_target_pairs={{0,8},{4,12},{8,16},{12,20},{16,24},{20,28},{24,0},{28,4},{1,9},{5... | collective-permute-start | bytes 786440 | tf_op jit(solution)/shard_map/ppermute | solution.py:60
  161.0 36.7 %collective-permute-start.2 = (bf16[256,512]{1,0:T(8,128)(2,1)}, bf16[256,512]{1,0:T(8,128)(2,1)}, u32[]{:S(2)}, u32[]{:S(2)}) collective-permute-start(bf16[256,512]{1,0:T(8,128)(2,1)} %get-tuple-element.51), channel_id=1, source_target_pairs={{0,24},{4,28},{8,0},{12,4},{16,8},{20,12},{24,16},{28,20},{1,25},{... | collective-permute-start | bytes 786440 | tf_op jit(solution)/shard_map/ppermute | solution.py:60
  163.3 52.9 %collective-permute-start.1 = (bf16[256,512]{1,0:T(8,128)(2,1)}, bf16[256,512]{1,0:T(8,128)(2,1)}, u32[]{:S(2)}, u32[]{:S(2)}) collective-permute-start(bf16[256,512]{1,0:T(8,128)(2,1)} %get-tuple-element.52), channel_id=1, source_target_pairs={{0,16},{4,20},{8,24},{12,28},{16,0},{20,4},{24,8},{28,12},{1,17},{... | collective-permute-start | bytes 786440 | tf_op jit(solution)/shard_map/ppermute | solution.py:60
  172.6 47.4 %collective-permute-start.21 = (bf16[128,2048]{1,0:T(8,128)(2,1)}, bf16[128,2048]{1,0:T(8,128)(2,1)S(1)}, u32[]{:S(2)}, u32[]{:S(2)}) collective-permute-start(bf16[128,2048]{1,0:T(8,128)(2,1)} %collective-permute-done.19), channel_id=1, source_target_pairs={{0,8},{4,12},{8,16},{12,20},{16,24},{20,28},{24,0},{28,4},{1,9},{5... | collective-permute-start | bytes 1572872 | tf_op jit(solution)/shard_map/ppermute | solution.py:60
  194.7 95.2 %all-gather.12.cloned.1.call-start = ((), (), s32[]{:S(2)}) async-start(), calls=%async_computation.16 | async-start | bytes 1310720 | tf_op jit(solution)/shard_map/all_gather | solution.py:102
  195.4 25.8 %collective-permute-start.20 = (bf16[128,2048]{1,0:T(8,128)(2,1)}, bf16[128,2048]{1,0:T(8,128)(2,1)}, u32[]{:S(2)}, u32[]{:S(2)}) collective-permute-start(bf16[128,2048]{1,0:T(8,128)(2,1)} %collective-permute-done.19), channel_id=1, source_target_pairs={{0,1},{1,0},{2,3},{3,2},{4,5},{5,4},{6,7},{7,6},{8,9},{9,8},{10,11... | collective-permute-start | bytes 1572872 | tf_op jit(solution)/shard_map/ppermute | solution.py:89
  196.6 248.4 %collective-permute-start.8 = (bf16[256,512]{0,1:T(8,128)(2,1)}, bf16[256,512]{0,1:T(8,128)(2,1)}, u32[]{:S(2)}, u32[]{:S(2)}) collective-permute-start(bf16[256,512]{0,1:T(8,128)(2,1)} %collective-permute-done.7), channel_id=1, source_target_pairs={{0,8},{4,12},{8,16},{12,20},{16,24},{20,28},{24,0},{28,4},{1,9},{5... | collective-permute-start | bytes 786440 | tf_op jit(solution)/shard_map/ppermute | solution.py:60
  272.6 80.9 %reduce-scatter.11.cloned.1.call-start = ((), (), s32[]{:S(2)}) async-start(), calls=%async_computation.17 | async-start | bytes 2621440 | tf_op jit(solution)/shard_map/reduce_scatter | solution.py:98
  344.1 56.5 %collective-permute-start.33 = (bf16[2048,256]{1,0:T(8,128)(2,1)}, bf16[2048,256]{1,0:T(8,128)(2,1)}, u32[]{:S(2)}, u32[]{:S(2)}) collective-permute-start(bf16[2048,256]{1,0:T(8,128)(2,1)} %fusion.9), channel_id=1, source_target_pairs={{0,4},{4,0},{8,12},{12,8},{16,20},{20,16},{24,28},{28,24},{1,5},{5... | collective-permute-start | bytes 3145736 | tf_op jit(solution)/shard_map/ppermute | solution.py:68
  345.7 30.0 %all-to-all-start = ((bf16[8,8,2048]{2,1,0:T(8,128)(2,1)}), bf16[8,8,2048]{2,1,0:T(8,128)(2,1)S(1)}, u32[]{:S(2)}, u32[]{:S(2)}) async-start(bf16[8,8,2048]{2,1,0:T(8,128)(2,1)} %get-tuple-element.37), calls=%async_computation.2 | async-start | bytes 524288 | tf_op jit(solution)/shard_map/all_to_all | solution.py:150
  351.5 50.1 %collective-permute-start.3 = (bf16[256,1536]{1,0:T(8,128)(2,1)}, bf16[256,1536]{1,0:T(8,128)(2,1)}, u32[]{:S(2)}, u32[]{:S(2)}) collective-permute-start(bf16[256,1536]{1,0:T(8,128)(2,1)} %pad_maximum_fusion.19), channel_id=1, source_target_pairs={{0,8},{4,12},{8,16},{12,20},{16,24},{20,28},{24,0},{28,4},{1,9},{5... | collective-permute-start | bytes 2359304 | tf_op jit(solution)/shard_map/ppermute | solution.py:60
  375.7 17.3 %all-to-all-start.4 = ((bf16[8,8,2048]{2,1,0:T(8,128)(2,1)}), bf16[8,8,2048]{2,1,0:T(8,128)(2,1)S(1)}, u32[]{:S(2)}, u32[]{:S(2)}) async-start(bf16[8,8,2048]{2,1,0:T(8,128)(2,1)} %fusion.48), calls=%async_computation.8 | async-start | bytes 524288 | tf_op jit(solution)/shard_map/all_to_all | solution.py:150
  383.8 49.7 %collective-permute-start.32 = (bf16[256,2048]{1,0:T(8,128)(2,1)}, bf16[256,2048]{1,0:T(8,128)(2,1)}, u32[]{:S(2)}, u32[]{:S(2)}) collective-permute-start(bf16[256,2048]{1,0:T(8,128)(2,1)} %fusion.8), channel_id=1, source_target_pairs={{0,4},{4,0},{8,12},{12,8},{16,20},{20,16},{24,28},{28,24},{1,5},{5... | collective-permute-start | bytes 3145736 | tf_op jit(solution)/shard_map/ppermute | solution.py:68
  392.2 55.2 %collective-permute-start.31 = (bf16[256,2048]{1,0:T(8,128)(2,1)}, bf16[256,2048]{1,0:T(8,128)(2,1)}, u32[]{:S(2)}, u32[]{:S(2)}) collective-permute-start(bf16[256,2048]{1,0:T(8,128)(2,1)} %fusion.7), channel_id=1, source_target_pairs={{0,4},{4,0},{8,12},{12,8},{16,20},{20,16},{24,28},{28,24},{1,5},{5... | collective-permute-start | bytes 3145736 | tf_op jit(solution)/shard_map/ppermute | solution.py:68
  394.6 38.2 %all-to-all-start.5 = ((bf16[8,8,2048]{2,1,0:T(8,128)(2,1)}), bf16[8,8,2048]{2,1,0:T(8,128)(2,1)S(1)}, u32[]{:S(2)}, u32[]{:S(2)}) async-start(bf16[8,8,2048]{2,1,0:T(8,128)(2,1)} %get-tuple-element.69), calls=%async_computation.9 | async-start | bytes 524288 | tf_op jit(solution)/shard_map/all_to_all | solution.py:150
  400.6 118.2 %all-gather.14.cloned.1.call-start = ((), (), s32[]{:S(2)}) async-start(), calls=%async_computation.18 | async-start | bytes 1310720 | tf_op jit(solution)/shard_map/all_gather | solution.py:102
  401.6 45.9 %collective-permute-start.4 = (bf16[256,1536]{1,0:T(8,128)(2,1)}, bf16[256,1536]{1,0:T(8,128)(2,1)}, u32[]{:S(2)}, u32[]{:S(2)}) collective-permute-start(bf16[256,1536]{1,0:T(8,128)(2,1)} %collective-permute-done.3), channel_id=1, source_target_pairs={{0,8},{4,12},{8,16},{12,20},{16,24},{20,28},{24,0},{28,4},{1,9},{5... | collective-permute-start | bytes 2359304 | tf_op jit(solution)/shard_map/ppermute | solution.py:60
  408.9 29.9 %collective-permute-start.16 = (f32[5123]{0:T(1024)S(1)}, f32[5123]{0:T(1024)S(1)}, u32[]{:S(2)}, u32[]{:S(2)}) collective-permute-start(f32[5123]{0:T(1024)S(1)} %concatenate.66), channel_id=1, source_target_pairs={{0,4},{4,0},{8,12},{12,8},{16,20},{20,16},{24,28},{28,24},{1,5},{5... | collective-permute-start | bytes 61484 | tf_op jit(solution)/shard_map/ppermute | solution.py:80
  440.5 40.4 %collective-permute-start.12 = (bf16[256,512]{1,0:T(8,128)(2,1)S(1)}, bf16[256,512]{1,0:T(8,128)(2,1)S(1)}, u32[]{:S(2)}, u32[]{:S(2)}) collective-permute-start(bf16[256,512]{1,0:T(8,128)(2,1)S(1)} %get-tuple-element.46), channel_id=1, source_target_pairs={{0,24},{4,28},{8,0},{12,4},{16,8},{20,12},{24,16},{28,20},{1,25},{... | collective-permute-start | bytes 786440 | tf_op jit(solution)/shard_map/ppermute | solution.py:60
  442.7 38.2 %collective-permute-start.11 = (bf16[256,512]{1,0:T(8,128)(2,1)S(1)}, bf16[256,512]{1,0:T(8,128)(2,1)S(1)}, u32[]{:S(2)}, u32[]{:S(2)}) collective-permute-start(bf16[256,512]{1,0:T(8,128)(2,1)S(1)} %get-tuple-element.47), channel_id=1, source_target_pairs={{0,16},{4,20},{8,24},{12,28},{16,0},{20,4},{24,8},{28,12},{1,17},{... | collective-permute-start | bytes 786440 | tf_op jit(solution)/shard_map/ppermute | solution.py:60
  445.1 35.8 %collective-permute-start.10 = (bf16[256,512]{1,0:T(8,128)(2,1)S(1)}, bf16[256,512]{1,0:T(8,128)(2,1)S(1)}, u32[]{:S(2)}, u32[]{:S(2)}) collective-permute-start(bf16[256,512]{1,0:T(8,128)(2,1)S(1)} %get-tuple-element.48), channel_id=1, source_target_pairs={{0,8},{4,12},{8,16},{12,20},{16,24},{20,28},{24,0},{28,4},{1,9},{5... | collective-permute-start | bytes 786440 | tf_op jit(solution)/shard_map/ppermute | solution.py:60
  447.4 32.9 %collective-permute-start.18 = (f32[5123]{0:T(1024)S(1)}, f32[5123]{0:T(1024)S(1)}, u32[]{:S(2)}, u32[]{:S(2)}) collective-permute-start(f32[5123]{0:T(1024)S(1)} %add.258), channel_id=1, source_target_pairs={{0,16},{4,20},{8,24},{12,28},{16,0},{20,4},{24,8},{28,12},{1,17},{... | collective-permute-start | bytes 61484 | tf_op jit(solution)/shard_map/ppermute | solution.py:80
  447.5 38.6 %collective-permute-start.5 = (bf16[256,1536]{1,0:T(8,128)(2,1)}, bf16[256,1536]{1,0:T(8,128)(2,1)}, u32[]{:S(2)}, u32[]{:S(2)}) collective-permute-start(bf16[256,1536]{1,0:T(8,128)(2,1)} %collective-permute-done.4), channel_id=1, source_target_pairs={{0,8},{4,12},{8,16},{12,20},{16,24},{20,28},{24,0},{28,4},{1,9},{5... | collective-permute-start | bytes 2359304 | tf_op jit(solution)/shard_map/ppermute | solution.py:60
  486.1 32.7 %all-gather.8.cloned.1.call-start = ((), (), s32[]{:S(2)}) async-start(), calls=%async_computation.13 | async-start | bytes 1310720 | tf_op jit(solution)/shard_map/all_gather | solution.py:102
  489.7 24.8 %collective-permute-start.6 = (bf16[256,1536]{1,0:T(8,128)(2,1)}, bf16[256,1536]{1,0:T(8,128)(2,1)}, u32[]{:S(2)}, u32[]{:S(2)}) collective-permute-start(bf16[256,1536]{1,0:T(8,128)(2,1)} %convolution_convert_fusion), channel_id=1, source_target_pairs={{0,4},{4,0},{8,12},{12,8},{16,20},{20,16},{24,28},{28,24},{1,5},{5... | collective-permute-start | bytes 2359304 | tf_op jit(solution)/shard_map/ppermute | solution.py:68
  493.2 18.9 %collective-permute-start.13 = (bf16[512,256]{1,0:T(8,128)(2,1)S(1)}, bf16[512,256]{1,0:T(8,128)(2,1)S(1)}, u32[]{:S(2)}, u32[]{:S(2)}) collective-permute-start(bf16[512,256]{1,0:T(8,128)(2,1)S(1)} %convolution_convert_fusion.1), channel_id=1, source_target_pairs={{0,4},{4,0},{8,12},{12,8},{16,20},{20,16},{24,28},{28,24},{1,5},{5... | collective-permute-start | bytes 786440 | tf_op jit(solution)/shard_map/ppermute | solution.py:68
  (96 other events, 1010.7 us)
Sparse Core Ops, SparseCore 0:
  45.5 31.7 reduce-scatter.4
  80.6 16.7 all-gather.5
  116.3 31.3 reduce-scatter.6
  153.7 16.7 all-gather.9
  194.8 31.8 reduce-scatter.8
  272.7 17.1 all-gather.11
  316.3 32.4 reduce-scatter.10
  433.6 15.9 all-gather.13
  495.3 16.0 all-gather.7

commit v2 on v1

v2 whole, which is shorter than its diff:
```python
import math

import jax
import jax.numpy as jnp
from jax import lax
from jax.experimental import pallas as pl
from jax.experimental.pallas import tpu as pltpu
from jax.sharding import PartitionSpec as P

D = 2048
HEAD = 128
EPS = 1e-06
F32 = jnp.float32
BF16 = jnp.bfloat16


def matmul(left, right):
    return jnp.dot(left, right, preferred_element_type=F32)


def left_inner(left, right):
    return lax.dot_general(left, right, (((0,), (0,)), ((), ())), preferred_element_type=F32)


def right_inner(left, right):
    return lax.dot_general(left, right, (((1,), (1,)), ((), ())), preferred_element_type=F32)


def rope_tables(rows, width):
    places = jnp.arange(rows, dtype=F32)
    freq = jnp.power(F32(500000.0), -jnp.arange(width // 2, dtype=F32) * (2.0 / width))
    angle = places[:, None] * freq[None, :]
    return (jnp.cos(angle), jnp.sin(angle))


class Grid:
    def __init__(self, count):
        self.count = count
        self.lanes = 2 ** ((count.bit_length() - 1) // 2)
        self.groups = count // self.lanes
        me = lax.axis_index("dp")
        self.group = me // self.lanes
        self.lane = me % self.lanes

    def shift_groups(self, field, step):
        pairs = [
            (g * self.lanes + a, ((g + step) % self.groups) * self.lanes + a)
            for g in range(self.groups)
            for a in range(self.lanes)
        ]
        return lax.ppermute(field, "dp", pairs)

    def shift_lanes(self, field, step):
        pairs = [
            (g * self.lanes + a, g * self.lanes + (a + step) % self.lanes)
            for g in range(self.groups)
            for a in range(self.lanes)
        ]
        return lax.ppermute(field, "dp", pairs)

    def ring(self, field):
        found = []
        for _ in range(self.groups - 1):
            field = self.shift_groups(field, 1)
            found.append(field)
        return found

    def total(self, field):
        step = 1
        while step < self.count:
            field = field + lax.ppermute(
                field, "dp", [(i, i ^ step) for i in range(self.count)]
            )
            step *= 2
        return field


def sibling(field):
    size = lax.axis_size("tensor")
    return lax.ppermute(field, "tensor", [(i, i ^ 1) for i in range(size)])


def across(field):
    size = lax.axis_size("tensor")
    return lax.ppermute(field, "tensor", [(i, (i + 2) % size) for i in range(size)])


def shared_ring(grid, rows_low):
    core = lax.axis_index("tensor") % 2
    half = rows_low.shape[0] // 2
    mine = lax.dynamic_slice_in_dim(rows_low, core * half, half, axis=0)
    pieces = []
    for piece in grid.ring(mine):
        pieces += [piece, sibling(piece)]
    return jnp.concatenate(pieces, axis=0)


SLOTS = 4
TILES = 2
AT = pl.DeviceIdType.MESH
VMEM_CAP = 56 * 2**20


class Team:
    def __init__(self):
        self.row = lax.axis_index("dp")
        self.me = lax.axis_index("tensor")
        self.side = self.me // 2
        self.core = self.me % 2
        self.slot = self.core * 2 + self.side
        self.sibling = self.side * 2 + (1 - self.core)
        self.across = (1 - self.side) * 2 + self.core
        self.far = (1 - self.side) * 2 + (1 - self.core)

    def meet(self, *others):
        barrier = pltpu.get_barrier_semaphore()
        for other in others:
            pl.semaphore_signal(barrier, inc=1, device_id=(self.row, other), device_id_type=AT)
        pl.semaphore_wait(barrier, len(others))

    def copy(self, source, target, send, recv, other):
        return pltpu.make_async_remote_copy(
            src_ref=source,
            dst_ref=target,
            send_sem=send,
            recv_sem=recv,
            device_id=(self.row, other),
            device_id_type=AT,
        )


def at_rows(start, size):
    return pl.ds(pl.multiple_of(start, size), size)


class Reduce:
    def scratch(rows, width):
        shard = rows // SLOTS
        return [
            pltpu.VMEM((rows, width), BF16),
            pltpu.VMEM((3, shard, width), BF16),
            pltpu.VMEM((shard, width), BF16),
            pltpu.VMEM((shard, width), F32),
            pltpu.SemaphoreType.DMA((3, TILES)),
            pltpu.SemaphoreType.DMA((3, TILES)),
        ]

    def __init__(self, team, partial, came, gone, total, send, recv):
        self.team, self.partial, self.came, self.gone, self.total = team, partial, came, gone, total
        self.shard, width = total.shape
        self.tile = width // TILES
        self.send, self.recv = send, recv
        self.copies = {}

    def columns(self, tile):
        return pl.ds(tile * self.tile, self.tile)

    def block(self, core, side):
        return at_rows((core * 2 + side) * self.shard, self.shard)

    def launch(self, kind, tile, source, other):
        copy = self.team.copy(
            source,
            self.came.at[kind, :, self.columns(tile)],
            self.send.at[kind, tile],
            self.recv.at[kind, tile],
            other,
        )
        copy.start()
        self.copies[kind, tile] = copy

    def offer(self, tile):
        team, columns = self.team, self.columns(tile)
        for kind, side in ((0, 1 - team.side), (1, team.side)):
            self.launch(
                kind, tile, self.partial.at[self.block(1 - team.core, side), columns], team.sibling
            )

    def pass_on(self, tile):
        team, columns = self.team, self.columns(tile)
        self.copies[0, tile].wait_recv()
        mine = self.partial[self.block(team.core, 1 - team.side), columns].astype(F32)
        self.gone[:, columns] = (mine + self.came[0, :, columns].astype(F32)).astype(BF16)
        self.launch(2, tile, self.gone.at[:, columns], team.across)

    def finish(self, tile):
        team, columns = self.team, self.columns(tile)
        self.copies[1, tile].wait_recv()
        mine = self.partial[self.block(team.core, team.side), columns].astype(F32)
        mine = mine + self.came[1, :, columns].astype(F32)
        self.copies[2, tile].wait_recv()
        self.total[:, columns] = mine + self.came[2, :, columns].astype(F32)

    def settle(self):
        for copy in self.copies.values():
            copy.wait_send()

    def run(self, make):
        for tile in range(TILES):
            make(tile)
            self.offer(tile)
            if tile:
                self.pass_on(tile - 1)
        self.pass_on(TILES - 1)
        for tile in range(TILES):
            self.finish(tile)
        self.settle()


class Gather:
    scratch = [pltpu.SemaphoreType.DMA((3,)), pltpu.SemaphoreType.DMA((3,))]

    def __init__(self, team, whole, send, recv):
        self.team, self.whole = team, whole
        shard = whole.shape[0] // SLOTS
        mine = whole.at[at_rows(team.slot * shard, shard)]
        theirs = whole.at[at_rows((team.core * 2 + 1 - team.side) * shard, shard)]
        self.across = team.copy(mine, mine, send.at[0], recv.at[0], team.across)
        self.near = team.copy(mine, mine, send.at[1], recv.at[1], team.sibling)
        self.relay = team.copy(theirs, theirs, send.at[2], recv.at[2], team.sibling)

    def start(self):
        self.across.start()
        self.near.start()

    def finish(self):
        self.across.wait_recv()
        self.relay.start()
        self.across.wait_send()
        self.near.wait()
        self.relay.wait()


class RowSums:
    def scratch(rows):
        return [
            pltpu.VMEM((8, rows), F32),
            pltpu.VMEM((3, 8, rows), F32),
            pltpu.SemaphoreType.DMA((3,)),
            pltpu.SemaphoreType.DMA((3,)),
        ]

    def __init__(self, team, mine, came, send, recv):
        self.team, self.mine, self.came = team, mine, came
        self.copies = [
            team.copy(mine, came.at[i], send.at[i], recv.at[i], other)
            for i, other in enumerate((team.sibling, team.across, team.far))
        ]

    def start(self, first, second):
        rows = first.shape[0]
        lane = lax.broadcasted_iota(jnp.int32, (rows, 128), 1)
        both = jnp.where(lane == 0, first, jnp.where(lane == 1, second, 0.0))
        self.mine[...] = jnp.transpose(both)[:8]
        for copy in self.copies:
            copy.start()

    def finish(self):
        for copy in self.copies:
            copy.wait()
        total = self.mine[...] + self.came[0] + (self.came[1] + self.came[2])
        rows = total.shape[1]
        wide = jnp.transpose(jnp.concatenate([total] * 16, axis=0))
        return wide[:, 0:1], wide[:, 1:2]


def turn(field, cosine, sine):
    return field * cosine + pltpu.roll(field, HEAD // 2, 1) * sine


def head_probs(queries, keys, length):
    rows = queries.shape[0]
    scores = right_inner(queries, keys) * (1.0 / math.sqrt(HEAD))
    row = lax.broadcasted_iota(jnp.int32, (rows, rows), 0)
    column = lax.broadcasted_iota(jnp.int32, (rows, rows), 1)
    masked = jnp.where((column <= row) & (column < length), scores, -1e30)
    expo = jnp.exp(masked - jnp.max(masked, axis=-1, keepdims=True))
    return expo / jnp.sum(expo, axis=-1, keepdims=True)


def row_sum(field):
    return jnp.sum(field, axis=-1, keepdims=True)


def over_rows(count, step, work):
    def one(i, carry):
        work(pl.ds(pl.multiple_of(i * step, step), step))
        return carry

    lax.fori_loop(0, count // step, one, 0)


def attend_kernel(
    length_ref,
    hidden,
    mine_hidden,
    q_weight,
    k_weight,
    v_weight,
    o_weight,
    q_gain,
    k_gain,
    cosine,
    sine,
    a_gain,
    q_raw,
    k_raw,
    queries,
    keys,
    values,
    scales,
    mix,
    branch,
    mid_low,
    weights,
    out_weight,
    load,
    *scratch,
):
    team = Team()
    sums = RowSums(team, *scratch[0:4])
    reduce = Reduce(team, *scratch[4:10])
    gather = Gather(team, mid_low, *scratch[10:12])
    loads = [
        pltpu.make_async_copy(source, weights.at[i], load.at[i])
        for i, source in enumerate((q_weight, k_weight, v_weight))
    ] + [pltpu.make_async_copy(o_weight, out_weight, load.at[3])]
    for one in loads:
        one.start()
    team.meet(team.sibling, team.across, team.far)
    rows, local = mix.shape
    width = mid_low.shape[1]
    length = length_ref[0]

    def project(i):
        loads[i].wait()
        return matmul(hidden[...], weights[i])

    q = project(0)
    q_raw[...] = q
    k = project(1)
    k_raw[...] = k
    sums.start(row_sum(q * q), row_sum(k * k))
    values[...] = project(2).astype(BF16)
    q_total, k_total = sums.finish()
    q_scale = lax.rsqrt(q_total * (1.0 / D) + EPS)
    k_scale = lax.rsqrt(k_total * (1.0 / D) + EPS)
    lane = lax.broadcasted_iota(jnp.int32, (rows, 128), 1)
    scales[...] = jnp.where(lane == 0, q_scale, k_scale)
    for head in range(local // HEAD):
        at = pl.ds(head * HEAD, HEAD)
        q = turn(q_raw[:, at] * q_scale * q_gain[:, at], cosine[...], sine[...]).astype(BF16)
        k = turn(k_raw[:, at] * k_scale * k_gain[:, at], cosine[...], sine[...]).astype(BF16)
        queries[:, at] = q
        keys[:, at] = k
        probs = head_probs(q, k, length).astype(BF16)
        mix[:, at] = matmul(probs, values[:, at]).astype(BF16)
    loads[3].wait()

    def make(tile):
        at = reduce.columns(tile)
        reduce.partial[:, at] = matmul(mix[...], out_weight[:, at]).astype(BF16)

    reduce.run(make)
    shard = reduce.shard

    def norm(at):
        part = reduce.total[at, :]
        branch[at, :] = part
        unit = part * lax.rsqrt(row_sum(part * part) * (1.0 / D) + EPS)
        mid = mine_hidden[at, :].astype(F32) + a_gain[...] * unit
        whole_at = pl.ds(pl.multiple_of(team.slot * shard + at.start, at.size), at.size)
        mid_low[whole_at, :] = mid.astype(BF16)

    over_rows(shard, 16, norm)
    gather.start()
    gather.finish()


ANY = pl.BlockSpec(memory_space=pl.ANY)
ON_CHIP = pl.BlockSpec(memory_space=pltpu.VMEM)
SCALAR = pl.BlockSpec(memory_space=pltpu.SMEM)


def shaped(*pairs):
    return tuple(jax.ShapeDtypeStruct(shape, kind) for shape, kind in pairs)


def attend(length, hidden, mine_hidden, weights, gains, cosine, sine, a_gain):
    rows, width = hidden.shape
    local = weights[0].shape[1]
    shard = rows // SLOTS
    return pl.pallas_call(
        attend_kernel,
        out_shape=shaped(
            ((rows, local), F32),
            ((rows, local), F32),
            ((rows, local), BF16),
            ((rows, local), BF16),
            ((rows, local), BF16),
            ((rows, 128), F32),
            ((rows, local), BF16),
            ((shard, width), F32),
            ((rows, width), BF16),
        ),
        in_specs=[SCALAR, ON_CHIP, ON_CHIP] + [ANY] * 4 + [ON_CHIP] * 5,
        out_specs=(ON_CHIP,) * 9,
        scratch_shapes=[
            pltpu.VMEM((3, width, local), BF16),
            pltpu.VMEM((local, width), BF16),
            pltpu.SemaphoreType.DMA((4,)),
        ]
        + RowSums.scratch(rows)
        + Reduce.scratch(rows, width)
        + Gather.scratch,
        compiler_params=pltpu.CompilerParams(
            collective_id=0, has_side_effects=True, vmem_limit_bytes=VMEM_CAP
        ),
        name="attend",
    )(length, hidden, mine_hidden, *weights, *gains, cosine, sine, a_gain)


def settle_kernel(
    length_ref,
    partial_in,
    mine_hidden,
    branch,
    grad_in,
    a_gain,
    m_gain,
    layer,
    d_mlp,
    m_gain_part,
    squares,
    *scratch,
):
    team = Team()
    reduce = Reduce(team, *scratch[0:6])
    gather = Gather(team, d_mlp, *scratch[6:8])
    team.meet(team.sibling, team.across)

    def make(tile):
        at = reduce.columns(tile)
        reduce.partial[:, at] = partial_in[:, at]

    reduce.run(make)
    shard = reduce.shard
    length = length_ref[0]
    m_gain_part[...] = jnp.zeros_like(m_gain_part)
    squares[...] = jnp.zeros_like(squares)

    def folded(field):
        return sum([field[8 * i : 8 * i + 8] for i in range(field.shape[0] // 8)])

    def norm(at):
        part = reduce.total[at, :]
        scale = lax.rsqrt(row_sum(part * part) * (1.0 / D) + EPS)
        unit = part * scale
        base = branch[at, :]
        a_unit = base * lax.rsqrt(row_sum(base * base) * (1.0 / D) + EPS)
        attn_out = a_gain[...] * a_unit
        mlp_out = m_gain[...] * unit
        rows_f = mine_hidden[at, :].astype(F32)
        row = team.slot * shard + at.start + lax.broadcasted_iota(jnp.int32, (at.size, 1), 0)
        live = row < length
        layer[at, :] = jnp.where(live, rows_f + attn_out + mlp_out, 0.0).astype(BF16)
        grad = jnp.where(live, grad_in[at, :].astype(F32), 0.0)
        m_gain_part[...] += folded(grad * unit)
        for i, field in enumerate((rows_f, attn_out, mlp_out)):
            squares[i] += folded(jnp.where(live, field * field, 0.0))
        scaled = grad * m_gain[...]
        back = scale * (scaled - unit * (row_sum(scaled * unit) * (1.0 / D)))
        whole_at = pl.ds(pl.multiple_of(team.slot * shard + at.start, at.size), at.size)
        d_mlp[whole_at, :] = back.astype(BF16)

    over_rows(shard, 16, norm)
    gather.start()
    gather.finish()


def settle(length, partial, mine_hidden, branch, grad_in, a_gain, m_gain):
    rows, width = partial.shape
    shard = rows // SLOTS
    return pl.pallas_call(
        settle_kernel,
        out_shape=shaped(
            ((shard, width), BF16),
            ((rows, width), BF16),
            ((8, width), F32),
            ((3, 8, width), F32),
        ),
        in_specs=[SCALAR] + [ON_CHIP] * 6,
        out_specs=(ON_CHIP,) * 4,
        scratch_shapes=Reduce.scratch(rows, width) + Gather.scratch,
        compiler_params=pltpu.CompilerParams(
            collective_id=1, has_side_effects=True, vmem_limit_bytes=VMEM_CAP
        ),
        name="settle",
    )(length, partial, mine_hidden, branch, grad_in, a_gain, m_gain)


def unattend_kernel(
    length_ref,
    partial_in,
    branch,
    grad_in,
    a_gain,
    o_weight,
    q_raw,
    k_raw,
    queries,
    keys,
    values,
    scales,
    q_gain,
    k_gain,
    cosine,
    sine,
    d_mid,
    a_gain_part,
    d_branch,
    d_heads,
    q_gain_part,
    k_gain_part,
    out_weight,
    d_mix,
    d_q,
    d_k,
    load,
    *scratch,
):
    team = Team()
    sums = RowSums(team, *scratch[0:4])
    reduce = Reduce(team, *scratch[4:10])
    gather = Gather(team, d_branch, *scratch[10:12])
    fetch = pltpu.make_async_copy(o_weight, out_weight, load.at[0])
    fetch.start()
    team.meet(team.sibling, team.across, team.far)
    rows, local = queries.shape

    def make(tile):
        at = reduce.columns(tile)
        reduce.partial[:, at] = partial_in[:, at]

    reduce.run(make)
    shard = reduce.shard
    length = length_ref[0]
    a_gain_part[...] = jnp.zeros_like(a_gain_part)

    def norm(at):
        row = team.slot * shard + at.start + lax.broadcasted_iota(jnp.int32, (at.size, 1), 0)
        grad = jnp.where(row < length, grad_in[at, :].astype(F32), 0.0) + reduce.total[at, :]
        d_mid[at, :] = grad
        base = branch[at, :]
        scale = lax.rsqrt(row_sum(base * base) * (1.0 / D) + EPS)
        unit = base * scale
        product = grad * unit
        a_gain_part[...] += sum([product[8 * i : 8 * i + 8] for i in range(at.size // 8)])
        scaled = grad * a_gain[...]
        back = scale * (scaled - unit * (row_sum(scaled * unit) * (1.0 / D)))
        whole_at = pl.ds(pl.multiple_of(team.slot * shard + at.start, at.size), at.size)
        d_branch[whole_at, :] = back.astype(BF16)

    over_rows(shard, 16, norm)
    gather.start()
    gather.finish()
    fetch.wait()
    d_mix[...] = right_inner(d_branch[...], out_weight[...]).astype(BF16)
    q_scale = scales[:, 0:1]
    k_scale = scales[:, 1:2]
    q_inner = jnp.zeros((rows, 1), F32)
    k_inner = jnp.zeros((rows, 1), F32)
    shrink = 1.0 / math.sqrt(HEAD)
    for head in range(local // HEAD):
        at = pl.ds(head * HEAD, HEAD)
        q, k, v, back = queries[:, at], keys[:, at], values[:, at], d_mix[:, at]
        probs = head_probs(q, k, length)
        d_probs = right_inner(back, v)
        d_scores = (probs * (d_probs - row_sum(probs * d_probs))).astype(BF16)
        d_heads[:, pl.ds(2 * local + head * HEAD, HEAD)] = left_inner(
            probs.astype(BF16), back
        ).astype(BF16)
        d_q_hat = turn(matmul(d_scores, k) * shrink, cosine[...], -sine[...])
        d_k_hat = turn(left_inner(d_scores, q) * shrink, cosine[...], -sine[...])
        q_unit = q_raw[:, at] * q_scale
        k_unit = k_raw[:, at] * k_scale
        q_gain_part[:, at] = jnp.sum(d_q_hat * q_unit, axis=0, keepdims=True)
        k_gain_part[:, at] = jnp.sum(d_k_hat * k_unit, axis=0, keepdims=True)
        q_scaled = d_q_hat * q_gain[:, at]
        k_scaled = d_k_hat * k_gain[:, at]
        d_q[:, at] = q_scaled
        d_k[:, at] = k_scaled
        q_inner += row_sum(q_scaled * q_unit)
        k_inner += row_sum(k_scaled * k_unit)
    sums.start(q_inner, k_inner)
    q_inner, k_inner = sums.finish()
    for i, (grad, raw, scale, inner) in enumerate(
        ((d_q, q_raw, q_scale, q_inner), (d_k, k_raw, k_scale, k_inner))
    ):
        factor = scale * scale * inner * (1.0 / D)
        d_heads[:, pl.ds(i * local, local)] = (scale * grad[...] - raw[...] * factor).astype(BF16)


def unattend(
    length, partial, branch, grad_in, a_gain, o_weight, kept, gains, cosine, sine
):
    rows, width = partial.shape
    local = o_weight.shape[0]
    shard = rows // SLOTS
    return pl.pallas_call(
        unattend_kernel,
        out_shape=shaped(
            ((shard, width), F32),
            ((8, width), F32),
            ((rows, width), BF16),
            ((rows, 3 * local), BF16),
            ((1, local), F32),
            ((1, local), F32),
        ),
        in_specs=[SCALAR] + [ON_CHIP] * 4 + [ANY] + [ON_CHIP] * 10,
        out_specs=(ON_CHIP,) * 6,
        scratch_shapes=[
            pltpu.VMEM((local, width), BF16),
            pltpu.VMEM((rows, local), BF16),
            pltpu.VMEM((rows, local), F32),
            pltpu.VMEM((rows, local), F32),
            pltpu.SemaphoreType.DMA((1,)),
        ]
        + RowSums.scratch(rows)
        + Reduce.scratch(rows, width)
        + Gather.scratch,
        compiler_params=pltpu.CompilerParams(
            collective_id=2, has_side_effects=True, vmem_limit_bytes=VMEM_CAP
        ),
        name="unattend",
    )(length, partial, branch, grad_in, a_gain, o_weight, *kept, *gains, cosine, sine)


class Deal:
    def __init__(self, count, shard, width):
        self.count = count
        self.columns = max(128, width // count)
        self.across = width // self.columns
        self.rows = shard * self.across // count

    def at(self, chunk, base=0):
        return (
            at_rows(base + (chunk // self.across) * self.rows, self.rows),
            at_rows((chunk % self.across) * self.columns, self.columns),
        )


def finish_kernel(
    length_ref,
    inverse,
    partial_in,
    d_mid,
    layer,
    layer_out,
    input_grad,
    closed,
    parked,
    leaving,
    deal_send,
    deal_recv,
    *scratch,
):
    team = Team()
    reduce = Reduce(team, *scratch[0:6])
    gathers = [
        Gather(team, whole, *scratch[6 + 2 * i : 8 + 2 * i])
        for i, whole in enumerate((layer_out, input_grad))
    ]
    count = lax.axis_size("dp")
    shard, width = d_mid.shape
    deal = Deal(count, shard, width)
    barrier = pltpu.get_barrier_semaphore()
    for step in range(1, count):
        pl.semaphore_signal(
            barrier, inc=1, device_id=(lax.rem(team.row + step, count), team.me), device_id_type=AT
        )
    for other in (team.sibling, team.across):
        pl.semaphore_signal(barrier, inc=1, device_id=(team.row, other), device_id_type=AT)
    pl.semaphore_wait(barrier, count + 1)

    def make(tile):
        at = reduce.columns(tile)
        reduce.partial[:, at] = partial_in[:, at]

    reduce.run(make)
    length = length_ref[0]

    def close(at):
        row = team.slot * shard + at.start + lax.broadcasted_iota(jnp.int32, (at.size, 1), 0)
        closed[at, :] = jnp.where(row < length, reduce.total[at, :] + d_mid[at, :], 0.0).astype(BF16)

    over_rows(shard, 16, close)

    def send(phase, step, i, source, target):
        return pltpu.make_async_remote_copy(
            src_ref=source,
            dst_ref=target,
            send_sem=deal_send.at[phase, step, i],
            recv_sem=deal_recv.at[phase, step, i],
            device_id=(lax.rem(team.row + step, count), team.me),
            device_id_type=AT,
        )

    first = []
    for i, source in enumerate((layer, closed)):
        for step in range(1, count):
            other = lax.rem(team.row + step, count)
            copy = send(0, step, i, source.at[deal.at(other)], parked.at[team.row, i])
            copy.start()
            first.append(copy)
        parked[team.row, i] = source[deal.at(team.row)]
    for copy in first:
        copy.wait()
    mine = team.slot * shard
    second = []
    for i, target in enumerate((layer_out, input_grad)):
        for step in range(1, count):
            other = lax.rem(team.row + step, count)
            leaving[other, i] = parked[inverse[other], i]
            copy = send(1, step, i, leaving.at[other, i], target.at[deal.at(team.row, mine)])
            copy.start()
            second.append(copy)
        target[deal.at(team.row, mine)] = parked[inverse[team.row], i]
    for copy in second:
        copy.wait()
    for gather in gathers:
        gather.start()
    for gather in gathers:
        gather.finish()


def close_layer(length, inverse, partial, d_mid, layer):
    rows, width = partial.shape
    shard = rows // SLOTS
    count = lax.axis_size("dp")
    deal = Deal(count, shard, width)
    chunk = (count, 2, deal.rows, deal.columns)
    return pl.pallas_call(
        finish_kernel,
        out_shape=shaped(((rows, width), BF16), ((rows, width), BF16)),
        in_specs=[SCALAR, SCALAR] + [ON_CHIP] * 3,
        out_specs=(ON_CHIP,) * 2,
        scratch_shapes=[
            pltpu.VMEM((shard, width), BF16),
            pltpu.VMEM(chunk, BF16),
            pltpu.VMEM(chunk, BF16),
            pltpu.SemaphoreType.DMA((2, count, 2)),
            pltpu.SemaphoreType.DMA((2, count, 2)),
        ]
        + Reduce.scratch(rows, width)
        + Gather.scratch * 2,
        compiler_params=pltpu.CompilerParams(
            collective_id=3, has_side_effects=True, vmem_limit_bytes=VMEM_CAP
        ),
        name="close_layer",
    )(length, inverse, partial, d_mid, layer)


def body(
    hidden_in,
    upstream_grad,
    seq_lengths,
    position_order,
    query_weight,
    key_weight,
    value_weight,
    output_weight,
    query_gain,
    key_gain,
    attn_gain,
    gate_weight,
    up_weight,
    down_weight,
    mlp_gain,
):
    count = lax.axis_size("dp")
    ways = lax.axis_size("tensor")
    myself = lax.axis_index("dp")
    part = lax.axis_index("tensor")
    grid = Grid(count)
    index = jnp.arange(count, dtype=jnp.int32)
    inverse = jnp.sum(
        index[None, :] * (position_order[None, :] == index[:, None]).astype(jnp.int32), axis=1
    )
    rows = hidden_in.shape[1]
    width = hidden_in.shape[2]
    shard = rows // ways
    piece = shard // count
    seq_here = jnp.sum(jnp.where(index == myself, position_order, 0))
    length = jnp.sum(jnp.where(index == seq_here, seq_lengths, 0))[None]
    slot = part % 2 * 2 + part // 2

    def exchange(pieces):
        return lax.all_to_all(pieces, "dp", split_axis=0, concat_axis=0, tiled=True)

    def my_rows(field):
        return lax.dynamic_slice_in_dim(field, slot * shard, shard, axis=0)

    first = exchange(my_rows(upstream_grad[0]).reshape(count, piece, width))
    second = exchange(jnp.take(first, position_order, axis=0))
    grad_in = second.reshape(shard, width)

    rows_low = hidden_in[0]
    my_low = my_rows(rows_low)
    local = query_weight.shape[1]
    strip = width // grid.groups
    tile = width // count

    def strip_of(field, group):
        return lax.dynamic_slice_in_dim(field, group * strip, strip, axis=1)

    def strips(field):
        found = [strip_of(field, grid.group)]
        for step in range(1, grid.groups):
            found.append(
                grid.shift_groups(
                    strip_of(field, (grid.group + step) % grid.groups), step
                )
            )
        return jnp.concatenate(found, axis=0)

    def tile_of(field, lane):
        return lax.dynamic_slice_in_dim(field, lane * tile, tile, axis=1)

    def reduced(product, field):
        sent = []
        for step in range(1, grid.lanes):
            other = product(tile_of(field, (grid.lane + step) % grid.lanes)).astype(BF16)
            sent.append(grid.shift_lanes(other, step))
        mine = product(tile_of(field, grid.lane))
        for other in sent:
            mine = mine + other.astype(F32)
        return mine

    hidden_strips = strips(rows_low)

    cosine, sine = rope_tables(rows, HEAD)
    cosine = jnp.concatenate([cosine, cosine], axis=1)
    sine = jnp.concatenate([-sine, sine], axis=1)
    gains = (query_gain[None], key_gain[None])
    q_raw, k_raw, queries, keys, values, scales, attn_mix, branch, mid_low = attend(
        length,
        rows_low,
        my_low,
        (query_weight, key_weight, value_weight, output_weight),
        gains,
        cosine,
        sine,
        attn_gain[None],
    )
    mix_all = jnp.concatenate([attn_mix] + grid.ring(attn_mix), axis=0)
    mid_others = shared_ring(grid, mid_low)

    gate = matmul(mid_low, gate_weight)
    upper = matmul(mid_low, up_weight)
    sig = jax.nn.sigmoid(gate)
    inner = (gate * sig * upper).astype(BF16)
    layer, d_mlp, mlp_gain_part, squares = settle(
        length,
        matmul(inner, down_weight).astype(BF16),
        my_low,
        branch,
        grad_in,
        attn_gain[None],
        mlp_gain[None],
    )
    d_mlp_others = shared_ring(grid, d_mlp)

    def inner_back(gate, upper, d_mlp):
        d_inner = right_inner(d_mlp, down_weight)
        sig = jax.nn.sigmoid(gate)
        d_gate = (d_inner * upper * sig * (1.0 + gate * (1.0 - sig))).astype(BF16)
        d_up = (d_inner * gate * sig).astype(BF16)
        return d_gate, d_up

    d_gate, d_up = inner_back(gate, upper, d_mlp)
    d_mid, attn_gain_part, d_branch, d_heads, query_gain_part, key_gain_part = unattend(
        length,
        (right_inner(d_gate, gate_weight) + right_inner(d_up, up_weight)).astype(BF16),
        branch,
        grad_in,
        attn_gain[None],
        output_weight,
        (q_raw, k_raw, queries, keys, values, scales),
        gains,
        cosine,
        sine,
    )
    d_branch_strips = strips(d_branch)
    d_heads_all = jnp.concatenate([d_heads] + grid.ring(d_heads), axis=0)
    layer_out, input_grad = close_layer(
        length,
        inverse,
        (
            right_inner(d_heads[:, :local], query_weight)
            + right_inner(d_heads[:, local : 2 * local], key_weight)
            + right_inner(d_heads[:, 2 * local :], value_weight)
        ).astype(BF16),
        d_mid,
        layer,
    )

    gate_o = matmul(mid_others, gate_weight)
    upper_o = matmul(mid_others, up_weight)
    inner_o = (jax.nn.silu(gate_o) * upper_o).astype(BF16)
    d_gate_o, d_up_o = inner_back(gate_o, upper_o, d_mlp_others)

    def strip_all(own, others):
        return jnp.concatenate([strip_of(own, grid.group), strip_of(others, grid.group)], axis=0)

    mid_strips = strip_all(mid_low, mid_others)
    d_mlp_strips = strip_all(d_mlp, d_mlp_others)
    d_gate_all = jnp.concatenate([d_gate, d_gate_o], axis=0)
    d_up_all = jnp.concatenate([d_up, d_up_o], axis=0)
    inner_all = jnp.concatenate([inner, inner_o], axis=0)
    gate_part = reduced(lambda tile: left_inner(tile, d_gate_all), mid_strips)
    up_part = reduced(lambda tile: left_inner(tile, d_up_all), mid_strips)
    down_part = reduced(lambda tile: left_inner(inner_all, tile), d_mlp_strips)
    output_part = reduced(lambda tile: left_inner(mix_all, tile), d_branch_strips)
    heads_part = reduced(lambda tile: left_inner(tile, d_heads_all), hidden_strips)
    query_part = heads_part[:, :local]
    key_part = heads_part[:, local : 2 * local]
    value_part = heads_part[:, 2 * local :]

    shared = jnp.concatenate(
        [jnp.sum(attn_gain_part, axis=0), jnp.sum(mlp_gain_part, axis=0), jnp.sum(squares, axis=(1, 2))]
    )
    shared = shared + sibling(shared)
    shared = shared + across(shared)
    sums = grid.total(jnp.concatenate([shared, query_gain_part[0], key_gain_part[0]]))
    attn_gain_grad = sums[:width]
    mlp_gain_grad = sums[width : 2 * width]
    squares = sums[2 * width : 2 * width + 3]
    query_gain_grad = sums[2 * width + 3 : 2 * width + 3 + local]
    key_gain_grad = sums[2 * width + 3 + local :]
    rms_values = jnp.sqrt(squares / (jnp.sum(seq_lengths).astype(F32) * D))

    return (
        layer_out[None],
        input_grad[None],
        query_part,
        key_part,
        value_part,
        output_part,
        query_gain_grad,
        key_gain_grad,
        attn_gain_grad,
        gate_part,
        up_part,
        down_part,
        mlp_gain_grad,
        rms_values,
    )


def solution(mesh):
    placed = (
        P("dp", None, None),
        P("dp", None, None),
        P(),
        P(),
        P(None, "tensor"),
        P(None, "tensor"),
        P(None, "tensor"),
        P("tensor", None),
        P("tensor"),
        P("tensor"),
        P(),
        P(None, "tensor"),
        P(None, "tensor"),
        P("tensor", None),
        P(),
    )
    return jax.shard_map(
        body,
        mesh=mesh,
        in_specs=placed,
        out_specs=(
            P("dp", None, None),
            P("dp", None, None),
            P("dp", "tensor"),
            P("dp", "tensor"),
            P("dp", "tensor"),
            P("tensor", "dp"),
            P("tensor"),
            P("tensor"),
            P(),
            P("dp", "tensor"),
            P("dp", "tensor"),
            P("tensor", "dp"),
            P(),
            P(),
        ),
        check_vma=False,
    )
```

time: 537 us -> 483 us (0.90)
  Pallas kernels: 0 us -> 134 us
  waiting for transfers between devices: 219 us -> 159 us
  matrix products: 136 us -> 91.4 us
  other arithmetic: 40.4 us -> 10.2 us
  local copies, waits for them, and re-layouts: 44 us -> 27.4 us
  blocking collectives: 14.3 us -> 0 us
  between operations: 16 us -> 2.52 us
  starting transfers between devices: 60.3 us -> 48.8 us
    pallas_call x0 -> x4, Pallas kernels: none -> 134 us  [the longest x1 50.2 us: close_layer(): pl.pallas_call(finish_kernel, out_shape=shaped(((rows, width), BF16), ((r...]
    ppermute x5, waiting for transfers between devices: 15.8 us -> 71 us  [shift_lanes(): return lax.ppermute(field, 'dp', pairs)]
    all_to_all x6 -> x2, waiting for transfers between devices: 52.1 us -> 0.01 us  [exchange(): return lax.all_to_all(pieces, 'dp', split_axis=0, concat_axis=0, tiled=True)]
    reduce_scatter x4 -> x0, waiting for transfers between devices: 38.9 us -> none  [reduce_rows(): return lax.psum_scatter(partial, 'tensor', scatter_dimension=0, tiled=True)]
    ppermute x3, waiting for transfers between devices: 27 us -> 1.29 us  [total(): lax.ppermute(field, 'dp', [(i, i ^ step) for i in range(self.count)])]
    dot_general x10, matrix products: 36.2 us -> 15.7 us  [left_inner(): lax.dot_general(left, right, (((0,), (0,)), ((), ())), preferred_element_...]
    all_gather x5 -> x0, waiting for transfers between devices: 19 us -> none  [gather_rows(): return lax.all_gather(shard, 'tensor', axis=0, tiled=True)]
    ppermute x18, waiting for transfers between devices: 64 us -> 82.9 us  [shift_groups(): return lax.ppermute(field, 'dp', pairs)]
  transfers between devices with their start and end apart: 49 -> 36, of which waited for: 18 -> 15; matrix products, arithmetic and copies ran while one was open for 29% -> 25% of each run, Pallas kernels for 0% -> 28%
where the time goes in v2:
time: 483 us; the launch traced here: 473 us
  waiting for transfers between devices  159 us (33%)
  Pallas kernels  134 us (28%)
  matrix products  91.4 us (19%)
  starting transfers between devices  48.8 us (10%)
  local copies, waits for them, and re-layouts  27.4 us (6%)
  other arithmetic  10.2 us (2%)
    ppermute x18, waiting for transfers between devices, shift_groups(): return lax.ppermute(field, 'dp', pairs)  82.9 us
    ppermute x5, waiting for transfers between devices, shift_lanes(): return lax.ppermute(field, 'dp', pairs)  71 us
    pallas_call x1, Pallas kernels, close_layer(): pl.pallas_call(finish_kernel, out_shape=shaped(((rows, width), BF16), ((r...  50.2 us
    dot_general x5, matrix products, matmul(): return jnp.dot(left, right, preferred_element_type=F32)  40.3 us
    dot_general x7, matrix products, right_inner(): lax.dot_general(left, right, (((1,), (1,)), ((), ())), preferred_element_...  35.5 us
    pallas_call x1, Pallas kernels, unattend(): pl.pallas_call(unattend_kernel, out_shape=shaped(((shard, width), F32), (...  31 us
    pallas_call x1, Pallas kernels, attend(): pl.pallas_call(attend_kernel, out_shape=shaped(((rows, local), F32), ((ro...  30.5 us
    ppermute x18, starting transfers between devices, shift_groups(): return lax.ppermute(field, 'dp', pairs)  24.7 us
  transfers between devices with their start and end apart: 36, of which 15 were waited for; matrix products, arithmetic and copies ran while one was open for 25% of the time, Pallas kernels for 28%

profile of v2, /device:TPU:0, one launch (start us, length us, event | category | flops | bytes accessed | tf_op | source)
XLA Modules:
  0.0 473.4 jit_solution(5653952368992416797)
XLA Ops:
  2.6 7.3 %all-to-all-start = ((bf16[8,8,2048]{2,1,0:T(8,128)(2,1)}), bf16[8,8,2048]{2,1,0:T(8,128)(2,1)S(1)}, u32[]{:S(2)}, u32[]{:S(2)}) async-start(bf16[8,8,2048]{2,1,0:T(8,128)(2,1)} %dynamic-slice_bitcast_fusion.4), calls=%async_computation | async-start | bytes 524288 | tf_op jit(solution)/shard_map/all_to_all | solution.py:799
  21.1 30.5 %attend.1 = (f32[256,512]{1,0:T(8,128)}, f32[256,512]{1,0:T(8,128)}, bf16[256,512]{1,0:T(8,128)(2,1)}, bf16[256,512]{1,0:T(8,128)(2,1)}, bf16[256,512]{1,0:T(8,1...) custom-call(s32[1]{0:T(128)} %bitcast.length_ref, ...), custom_call_target="tpu_custom_call" | custom-call | tf_op jit(solution)/shard_map/attend/pallas_call | solution.py:393
  59.4 6.2 %fusion.54 = f32[256,2048]{1,0:T(8,128)S(1)} fusion(bf16[256,2048]{1,0:T(8,128)(2,1)} %get-tuple-element.35, bf16[2048,2048]{1,0:T(8,128)(2,1)} %param.26), kind=kOutput, calls=%fused_computation.129 | convolution fusion | flops 2147483648 | bytes 11534336 | tf_op jit(solution)/shard_map/dot_general | solution.py:18
  65.6 3.9 multiply_convert_fusion.5
  69.5 3.3 convolution_convert_fusion.1.partial_in
  76.9 6.3 %all-to-all-start.1 = ((bf16[8,8,2048]{2,1,0:T(8,128)(2,1)}), bf16[8,8,2048]{2,1,0:T(8,128)(2,1)S(1)}, u32[]{:S(2)}, u32[]{:S(2)}) async-start(bf16[8,8,2048]{2,1,0:T(8,128)(2,1)} %broadcast_select_fusion), calls=%async_computation.1 | async-start | bytes 524288 | tf_op jit(solution)/shard_map/all_to_all | solution.py:799
  89.8 18.3 %collective-permute-done.9 = bf16[256,512]{1,0:T(8,128)(2,1)S(1)} collective-permute-done((bf16[256,512]{1,0:T(8,128)(2,1)S(1)}, bf16[256,512]{1,0:T(8,128)(2,1)S(1)}, u32[]{:S(2)}, u32[]{:S(2)}) %collective-permute-start.9) | collective-permute-done | bytes 262176 | tf_op jit(solution)/shard_map/ppermute | solution.py:51
  109.5 22.5 %settle.1 = (bf16[64,2048]{1,0:T(8,128)(2,1)}, bf16[256,2048]{1,0:T(8,128)(2,1)}, f32[8,2048]{1,0:T(8,128)}, f32[3,8,2048]{2,1,0:T(8,128)}) custom-call(s32[1]{0:T(128)} %bitcast.length_ref, bf16[256,2048]{1,0:T(8,128)(2,1)} %convolution_convert_fusion.1.partial_in, bf16[64,2048]{1,0:T(8,128)(2,1)} %dynamic-slice_bitcast_fusion.5.mine_hidden, ...), custom_call_target="tpu_custom_call" | custom-call | tf_op jit(solution)/shard_map/settle/pallas_call | solution.py:484
  133.9 7.8 %multiply_convert_fusion.3 = (bf16[256,2048]{1,0:T(8,128)(2,1)S(1)}, bf16[256,2048]{1,0:T(8,128)(2,1)S(1)}) fusion(f32[256,2048]{1,0:T(8,128)} %copy-done.24, f32[256,2048]{1,0:T(8,128)} %get-tuple-element.84, bf16[256,2048]{1,0:T(8,128)(2,1)} %get-tuple-element.37, bf16[2048,2048]{1,0:T(8,128)(2,1)} %param.28), kind=kOutput, calls=%fused_computation.28 | convolution fusion | flops 2154299392 | bytes 15728640 | tf_op jit(solution)/shard_map/dot_general | solution.py:26
  141.8 6.5 %fusion.55 = f32[256,2048]{1,0:T(8,128)S(1)} fusion(bf16[256,2048]{1,0:T(8,128)(2,1)S(1)} %get-tuple-element.62, bf16[2048,2048]{1,0:T(8,128)(2,1)} %param.26), kind=kOutput, calls=%fused_computation.130 | convolution fusion | flops 2147483648 | bytes 11534336 | tf_op jit(solution)/shard_map/dot_general | solution.py:26
  148.3 6.8 %fusion.6.partial_in = bf16[256,2048]{1,0:T(8,128)(2,1)} fusion(f32[256,2048]{1,0:T(8,128)S(1)} %fusion.55, bf16[256,2048]{1,0:T(8,128)(2,1)S(1)} %get-tuple-element.61, bf16[2048,2048]{1,0:T(8,128)(2,1)} %param.27), kind=kOutput, calls=%fused_computation.18 | convolution fusion | flops 2148532224 | bytes 12582912 | tf_op jit(solution)/shard_map/dot_general | solution.py:26
  155.1 31.0 %unattend.1 = (f32[64,2048]{1,0:T(8,128)}, f32[8,2048]{1,0:T(8,128)}, bf16[256,2048]{1,0:T(8,128)(2,1)}, bf16[256,1536]{1,0:T(8,128)(2,1)}, f32[1,512]{1,0:T(1,128)}, /*index=5*/f32[1,512]{1,0:T(1,128)}) custom-call(s32[1]{0:T(128)} %bitcast.length_ref, bf16[256,2048]{1,0:T(8,128)(2,1)} %fusion.6.partial_in, f32[64,2048]{1,0:T(8,128)} %get-tuple-element.36.branch, ...), custom_call_target="tpu_custom_call" | custom-call | tf_op jit(solution)/shard_map/unattend/pallas_call | solution.py:610
  201.8 3.3 collective-permute-start.12
  206.6 3.3 fusion.10.partial_in
  209.9 50.2 %close_layer.1 = (bf16[256,2048]{1,0:T(8,128)(2,1)}, bf16[256,2048]{1,0:T(8,128)(2,1)}) custom-call(s32[1]{0:T(128)} %bitcast.length_ref, s32[8]{0:T(128)} %select_reduce_fusion.inverse, bf16[256,2048]{1,0:T(8,128)(2,1)} %fusion.10.partial_in, f32[64,2048]{1,0:T(8,128)} %get-tuple-element.45.d_mid, bf16[64,2048]{1,0:T(8,128)(2,1)} %get-tuple-element.46.layer), custom_call_target="tpu_custom_call" | custom-call | tf_op jit(solution)/shard_map/close_layer/pallas_call | solution.py:743
  260.2 3.7 collective-permute-start.10
  269.0 2.9 collective-permute-start.25
  272.0 3.0 collective-permute-done.10
  279.0 24.1 %collective-permute-done.25 = bf16[128,2048]{1,0:T(8,128)(2,1)S(1)} collective-permute-done((bf16[128,2048]{1,0:T(8,128)(2,1)S(1)}, bf16[128,2048]{1,0:T(8,128)(2,1)S(1)}, u32[]{:S(2)}, u32[]{:S(2)}) %collective-permute-start.25) | collective-permute-done | bytes 524320 | tf_op jit(solution)/shard_map/ppermute | solution.py:51
  304.4 9.8 %collective-permute-done.23 = bf16[128,2048]{1,0:T(8,128)(2,1)S(1)} collective-permute-done((bf16[128,2048]{1,0:T(8,128)(2,1)}, bf16[128,2048]{1,0:T(8,128)(2,1)S(1)}, u32[]{:S(2)}, u32[]{:S(2)}) %collective-permute-start.23) | collective-permute-done | bytes 524320 | tf_op jit(solution)/shard_map/ppermute | solution.py:51
  314.5 11.0 %collective-permute-done.27 = bf16[128,2048]{1,0:T(8,128)(2,1)S(1)} collective-permute-done((bf16[128,2048]{1,0:T(8,128)(2,1)S(1)}, bf16[128,2048]{1,0:T(8,128)(2,1)S(1)}, u32[]{:S(2)}, u32[]{:S(2)}) %collective-permute-start.27) | collective-permute-done | bytes 524320 | tf_op jit(solution)/shard_map/ppermute | solution.py:51
  325.7 11.1 %fusion.57 = f32[768,2048]{1,0:T(8,128)} fusion(bf16[768,2048]{1,0:T(8,128)(2,1)S(1)} %constant_dynamic-update-slice_fusion.8, bf16[2048,2048]{1,0:T(8,128)(2,1)} %param.26), kind=kOutput, calls=%fused_computation.132 | convolution fusion | flops 6442450944 | bytes 17825792 | tf_op jit(solution)/shard_map/dot_general | solution.py:18
  336.9 5.5 %collective-permute-done.4 = bf16[256,1536]{1,0:T(8,128)(2,1)S(1)} collective-permute-done((bf16[256,1536]{1,0:T(8,128)(2,1)S(1)}, bf16[256,1536]{1,0:T(8,128)(2,1)S(1)}, u32[]{:S(2)}, u32[]{:S(2)}) %collective-permute-start.4) | collective-permute-done | bytes 786464 | tf_op jit(solution)/shard_map/ppermute | solution.py:51
  342.4 11.2 %collective-permute-done.29 = bf16[128,2048]{1,0:T(8,128)(2,1)S(1)} collective-permute-done((bf16[128,2048]{1,0:T(8,128)(2,1)S(1)}, bf16[128,2048]{1,0:T(8,128)(2,1)S(1)}, u32[]{:S(2)}, u32[]{:S(2)}) %collective-permute-start.29) | collective-permute-done | bytes 524320 | tf_op jit(solution)/shard_map/ppermute | solution.py:51
  355.6 8.7 %fusion.56 = f32[768,2048]{1,0:T(8,128)} fusion(bf16[768,2048]{1,0:T(8,128)(2,1)S(1)} %constant_dynamic-update-slice_fusion.14, bf16[2048,2048]{1,0:T(8,128)(2,1)S(1)} %bitcast.66), kind=kOutput, calls=%fused_computation.131 | convolution fusion | flops 6442450944 | bytes 17825792 | tf_op jit(solution)/shard_map/dot_general | solution.py:26
  364.3 15.9 %multiply_convert_fusion = (bf16[768,2048]{1,0:T(8,128)(2,1)}, bf16[768,2048]{1,0:T(8,128)(2,1)S(1)}, bf16[768,2048]{1,0:T(8,128)(2,1)}) fusion(f32[768,2048]{1,0:T(8,128)} %fusion.57, f32[768,2048]{1,0:T(8,128)} %fusion.56, bf16[768,2048]{1,0:T(8,128)(2,1)S(1)} %constant_dynamic-update-slice_fusion.8, bf16[2048,2048]{1,0:T(8,128)(2,1)} %param.27), kind=kOutput, calls=%fused_computation.1 | convolution fusion | flops 6467616768 | bytes 33554432 | tf_op jit(solution)/shard_map/dot_general | solution.py:18
  389.9 11.8 %collective-permute-done.6 = bf16[256,1536]{1,0:T(8,128)(2,1)S(1)} collective-permute-done((bf16[256,1536]{1,0:T(8,128)(2,1)S(1)}, bf16[256,1536]{1,0:T(8,128)(2,1)S(1)}, u32[]{:S(2)}, u32[]{:S(2)}) %collective-permute-start.6) | collective-permute-done | bytes 786464 | tf_op jit(solution)/shard_map/ppermute | solution.py:59
  403.9 20.3 %collective-permute-done.32 = bf16[256,2048]{1,0:T(8,128)(2,1)S(1)} collective-permute-done((bf16[256,2048]{1,0:T(8,128)(2,1)S(1)}, bf16[256,2048]{1,0:T(8,128)(2,1)S(1)}, u32[]{:S(2)}, u32[]{:S(2)}) %collective-permute-start.32) | collective-permute-done | bytes 1048608 | tf_op jit(solution)/shard_map/ppermute | solution.py:59
  426.8 19.9 %collective-permute-done.31 = bf16[256,2048]{1,0:T(8,128)(2,1)S(1)} collective-permute-done((bf16[256,2048]{1,0:T(8,128)(2,1)S(1)}, bf16[256,2048]{1,0:T(8,128)(2,1)S(1)}, u32[]{:S(2)}, u32[]{:S(2)}) %collective-permute-start.31) | collective-permute-done | bytes 1048608 | tf_op jit(solution)/shard_map/ppermute | solution.py:59
  446.6 2.6 convert_add_fusion.2
  449.3 19.1 %collective-permute-done.33 = bf16[2048,256]{1,0:T(8,128)(2,1)S(1)} collective-permute-done((bf16[2048,256]{1,0:T(8,128)(2,1)S(1)}, bf16[2048,256]{1,0:T(8,128)(2,1)S(1)}, u32[]{:S(2)}, u32[]{:S(2)}) %collective-permute-start.33) | collective-permute-done | bytes 1048608 | tf_op jit(solution)/shard_map/ppermute | solution.py:59
  468.3 2.7 convert_add_fusion
  (193 shorter events, 80.7 us)
Async XLA Ops:
  2.6 72.9 %all-to-all-start = ((bf16[8,8,2048]{2,1,0:T(8,128)(2,1)}), bf16[8,8,2048]{2,1,0:T(8,128)(2,1)S(1)}, u32[]{:S(2)}, u32[]{:S(2)}) async-start(bf16[8,8,2048]{2,1,0:T(8,128)(2,1)} %dynamic-slice_bitcast_fusion.4), calls=%async_computation | async-start | bytes 524288 | tf_op jit(solution)/shard_map/all_to_all | solution.py:799
  11.1 62.6 %collective-permute-start = (bf16[256,512]{1,0:T(8,128)(2,1)S(1)}, bf16[256,512]{1,0:T(8,128)(2,1)S(1)}, u32[]{:S(2)}, u32[]{:S(2)}) collective-permute-start(bf16[256,512]{1,0:T(8,128)(2,1)S(1)} %get-tuple-element.71), channel_id=1, source_target_pairs={{0,8},{4,12},{8,16},{12,20},{16,24},{20,28},{24,0},{28,4},{1,9},{5... | collective-permute-start | bytes 786440 | tf_op jit(solution)/shard_map/ppermute | solution.py:51
  13.2 60.5 %collective-permute-start.2 = (bf16[256,512]{1,0:T(8,128)(2,1)S(1)}, bf16[256,512]{1,0:T(8,128)(2,1)S(1)}, u32[]{:S(2)}, u32[]{:S(2)}) collective-permute-start(bf16[256,512]{1,0:T(8,128)(2,1)S(1)} %get-tuple-element.72), channel_id=1, source_target_pairs={{0,24},{4,28},{8,0},{12,4},{16,8},{20,12},{24,16},{28,20},{1,25},{... | collective-permute-start | bytes 786440 | tf_op jit(solution)/shard_map/ppermute | solution.py:51
  15.1 58.6 %collective-permute-start.1 = (bf16[256,512]{1,0:T(8,128)(2,1)S(1)}, bf16[256,512]{1,0:T(8,128)(2,1)S(1)}, u32[]{:S(2)}, u32[]{:S(2)}) collective-permute-start(bf16[256,512]{1,0:T(8,128)(2,1)S(1)} %get-tuple-element.73), channel_id=1, source_target_pairs={{0,16},{4,20},{8,24},{12,28},{16,0},{20,4},{24,8},{28,12},{1,17},{... | collective-permute-start | bytes 786440 | tf_op jit(solution)/shard_map/ppermute | solution.py:51
  51.6 21.9 %collective-permute-start.7 = (bf16[256,512]{1,0:T(8,128)(2,1)}, bf16[256,512]{1,0:T(8,128)(2,1)S(1)}, u32[]{:S(2)}, u32[]{:S(2)}) collective-permute-start(bf16[256,512]{1,0:T(8,128)(2,1)} %get-tuple-element.49), channel_id=1, source_target_pairs={{0,8},{4,12},{8,16},{12,20},{16,24},{20,28},{24,0},{28,4},{1,9},{5... | collective-permute-start | bytes 786440 | tf_op jit(solution)/shard_map/ppermute | solution.py:51
  54.2 29.0 %collective-permute-start.19 = (bf16[128,2048]{1,0:T(8,128)(2,1)S(1)}, bf16[128,2048]{1,0:T(8,128)(2,1)}, u32[]{:S(2)}, u32[]{:S(2)}) collective-permute-start(bf16[128,2048]{1,0:T(8,128)(2,1)S(1)} %constant_dynamic-slice_fusion.4), channel_id=1, source_target_pairs={{0,8},{4,12},{8,16},{12,20},{16,24},{20,28},{24,0},{28,4},{1,9},{5... | collective-permute-start | bytes 1572872 | tf_op jit(solution)/shard_map/ppermute | solution.py:51
  73.5 12.2 %collective-permute-start.8 = (bf16[256,512]{1,0:T(8,128)(2,1)S(1)}, bf16[256,512]{1,0:T(8,128)(2,1)S(1)}, u32[]{:S(2)}, u32[]{:S(2)}) collective-permute-start(bf16[256,512]{1,0:T(8,128)(2,1)S(1)} %collective-permute-done.7), channel_id=1, source_target_pairs={{0,8},{4,12},{8,16},{12,20},{16,24},{20,28},{24,0},{28,4},{1,9},{5... | collective-permute-start | bytes 786440 | tf_op jit(solution)/shard_map/ppermute | solution.py:51
  76.9 32.0 %all-to-all-start.1 = ((bf16[8,8,2048]{2,1,0:T(8,128)(2,1)}), bf16[8,8,2048]{2,1,0:T(8,128)(2,1)S(1)}, u32[]{:S(2)}, u32[]{:S(2)}) async-start(bf16[8,8,2048]{2,1,0:T(8,128)(2,1)} %broadcast_select_fusion), calls=%async_computation.1 | async-start | bytes 524288 | tf_op jit(solution)/shard_map/all_to_all | solution.py:799
  83.2 185.7 %collective-permute-start.21 = (bf16[128,2048]{1,0:T(8,128)(2,1)}, bf16[128,2048]{1,0:T(8,128)(2,1)}, u32[]{:S(2)}, u32[]{:S(2)}) collective-permute-start(bf16[128,2048]{1,0:T(8,128)(2,1)} %collective-permute-done.19), channel_id=1, source_target_pairs={{0,8},{4,12},{8,16},{12,20},{16,24},{20,28},{24,0},{28,4},{1,9},{5... | collective-permute-start | bytes 1572872 | tf_op jit(solution)/shard_map/ppermute | solution.py:51
  85.7 180.0 %collective-permute-start.20 = (bf16[128,2048]{1,0:T(8,128)(2,1)}, bf16[128,2048]{1,0:T(8,128)(2,1)}, u32[]{:S(2)}, u32[]{:S(2)}) collective-permute-start(bf16[128,2048]{1,0:T(8,128)(2,1)} %collective-permute-done.19), channel_id=1, source_target_pairs={{0,1},{1,0},{2,3},{3,2},{4,5},{5,4},{6,7},{7,6},{8,9},{9,8},{10,11... | collective-permute-start | bytes 1572872 | tf_op jit(solution)/shard_map/ppermute | solution.py:80
  85.7 22.4 %collective-permute-start.9 = (bf16[256,512]{1,0:T(8,128)(2,1)S(1)}, bf16[256,512]{1,0:T(8,128)(2,1)S(1)}, u32[]{:S(2)}, u32[]{:S(2)}) collective-permute-start(bf16[256,512]{1,0:T(8,128)(2,1)S(1)} %collective-permute-done.8), channel_id=1, source_target_pairs={{0,8},{4,12},{8,16},{12,20},{16,24},{20,28},{24,0},{28,4},{1,9},{5... | collective-permute-start | bytes 786440 | tf_op jit(solution)/shard_map/ppermute | solution.py:51
  186.9 5.7 %collective-permute-start.14 = (f32[4099]{0:T(1024)S(1)}, f32[4099]{0:T(1024)S(1)}, u32[]{:S(2)}, u32[]{:S(2)}) collective-permute-start(f32[4099]{0:T(1024)S(1)} %pad_maximum_fusion.21), channel_id=1, source_target_pairs={{0,1},{1,0},{2,3},{3,2},{4,5},{5,4},{6,7},{7,6},{8,9},{9,8},{10,11... | collective-permute-start | bytes 49196 | tf_op jit(solution)/shard_map/ppermute | solution.py:80
  189.3 82.6 %collective-permute-start.11 = (bf16[256,512]{1,0:T(8,128)(2,1)}, bf16[256,512]{1,0:T(8,128)(2,1)}, u32[]{:S(2)}, u32[]{:S(2)}) collective-permute-start(bf16[256,512]{1,0:T(8,128)(2,1)} %get-tuple-element.68), channel_id=1, source_target_pairs={{0,16},{4,20},{8,24},{12,28},{16,0},{20,4},{24,8},{28,12},{1,17},{... | collective-permute-start | bytes 786440 | tf_op jit(solution)/shard_map/ppermute | solution.py:51
  201.8 70.1 %collective-permute-start.12 = (bf16[256,512]{1,0:T(8,128)(2,1)}, bf16[256,512]{1,0:T(8,128)(2,1)}, u32[]{:S(2)}, u32[]{:S(2)}) collective-permute-start(bf16[256,512]{1,0:T(8,128)(2,1)} %get-tuple-element.67), channel_id=1, source_target_pairs={{0,24},{4,28},{8,0},{12,4},{16,8},{20,12},{24,16},{28,20},{1,25},{... | collective-permute-start | bytes 786440 | tf_op jit(solution)/shard_map/ppermute | solution.py:51
  205.3 54.9 %collective-permute-start.18 = (f32[5123]{0:T(1024)S(1)}, f32[5123]{0:T(1024)S(1)}, u32[]{:S(2)}, u32[]{:S(2)}) collective-permute-start(f32[5123]{0:T(1024)S(1)} %add.181), channel_id=1, source_target_pairs={{0,16},{4,20},{8,24},{12,28},{16,0},{20,4},{24,8},{28,12},{1,17},{... | collective-permute-start | bytes 61484 | tf_op jit(solution)/shard_map/ppermute | solution.py:71
  260.2 14.7 %collective-permute-start.10 = (bf16[256,512]{1,0:T(8,128)(2,1)S(1)}, bf16[256,512]{1,0:T(8,128)(2,1)S(1)}, u32[]{:S(2)}, u32[]{:S(2)}) collective-permute-start(bf16[256,512]{1,0:T(8,128)(2,1)S(1)} %get-tuple-element.69), channel_id=1, source_target_pairs={{0,8},{4,12},{8,16},{12,20},{16,24},{20,28},{24,0},{28,4},{1,9},{5... | collective-permute-start | bytes 786440 | tf_op jit(solution)/shard_map/ppermute | solution.py:51
  265.7 48.6 %collective-permute-start.3 = (bf16[256,1536]{1,0:T(8,128)(2,1)S(1)}, bf16[256,1536]{1,0:T(8,128)(2,1)S(1)}, u32[]{:S(2)}, u32[]{:S(2)}) collective-permute-start(bf16[256,1536]{1,0:T(8,128)(2,1)S(1)} %copy-done.5), channel_id=1, source_target_pairs={{0,8},{4,12},{8,16},{12,20},{16,24},{20,28},{24,0},{28,4},{1,9},{5... | collective-permute-start | bytes 2359304 | tf_op jit(solution)/shard_map/ppermute | solution.py:51
  269.0 34.1 %collective-permute-start.25 = (bf16[128,2048]{1,0:T(8,128)(2,1)S(1)}, bf16[128,2048]{1,0:T(8,128)(2,1)S(1)}, u32[]{:S(2)}, u32[]{:S(2)}) collective-permute-start(bf16[128,2048]{1,0:T(8,128)(2,1)S(1)} %constant_dynamic-slice_fusion.2), channel_id=1, source_target_pairs={{0,8},{4,12},{8,16},{12,20},{16,24},{20,28},{24,0},{28,4},{1,9},{5... | collective-permute-start | bytes 1572872 | tf_op jit(solution)/shard_map/ppermute | solution.py:51
  271.9 42.4 %collective-permute-start.23 = (bf16[128,2048]{1,0:T(8,128)(2,1)}, bf16[128,2048]{1,0:T(8,128)(2,1)S(1)}, u32[]{:S(2)}, u32[]{:S(2)}) collective-permute-start(bf16[128,2048]{1,0:T(8,128)(2,1)} %collective-permute-done.21), channel_id=1, source_target_pairs={{0,8},{4,12},{8,16},{12,20},{16,24},{20,28},{24,0},{28,4},{1,9},{5... | collective-permute-start | bytes 1572872 | tf_op jit(solution)/shard_map/ppermute | solution.py:51
  272.0 42.3 %collective-permute-start.22 = (bf16[128,2048]{1,0:T(8,128)(2,1)}, bf16[128,2048]{1,0:T(8,128)(2,1)S(1)}, u32[]{:S(2)}, u32[]{:S(2)}) collective-permute-start(bf16[128,2048]{1,0:T(8,128)(2,1)} %collective-permute-done.21), channel_id=1, source_target_pairs={{0,1},{1,0},{2,3},{3,2},{4,5},{5,4},{6,7},{7,6},{8,9},{9,8},{10,11... | collective-permute-start | bytes 1572872 | tf_op jit(solution)/shard_map/ppermute | solution.py:80
  276.6 26.5 %collective-permute-start.13 = (bf16[512,256]{1,0:T(8,128)(2,1)S(1)}, bf16[512,256]{1,0:T(8,128)(2,1)S(1)}, u32[]{:S(2)}, u32[]{:S(2)}) collective-permute-start(bf16[512,256]{1,0:T(8,128)(2,1)S(1)} %convolution_convert_fusion.2), channel_id=1, source_target_pairs={{0,4},{4,0},{8,12},{12,8},{16,20},{20,16},{24,28},{28,24},{1,5},{5... | collective-permute-start | bytes 786440 | tf_op jit(solution)/shard_map/ppermute | solution.py:59
  303.0 22.5 %collective-permute-start.27 = (bf16[128,2048]{1,0:T(8,128)(2,1)S(1)}, bf16[128,2048]{1,0:T(8,128)(2,1)S(1)}, u32[]{:S(2)}, u32[]{:S(2)}) collective-permute-start(bf16[128,2048]{1,0:T(8,128)(2,1)S(1)} %collective-permute-done.25), channel_id=1, source_target_pairs={{0,8},{4,12},{8,16},{12,20},{16,24},{20,28},{24,0},{28,4},{1,9},{5... | collective-permute-start | bytes 1572872 | tf_op jit(solution)/shard_map/ppermute | solution.py:51
  303.1 22.4 %collective-permute-start.26 = (bf16[128,2048]{1,0:T(8,128)(2,1)S(1)}, bf16[128,2048]{1,0:T(8,128)(2,1)S(1)}, u32[]{:S(2)}, u32[]{:S(2)}) collective-permute-start(bf16[128,2048]{1,0:T(8,128)(2,1)S(1)} %collective-permute-done.25), channel_id=1, source_target_pairs={{0,1},{1,0},{2,3},{3,2},{4,5},{5,4},{6,7},{7,6},{8,9},{9,8},{10,11... | collective-permute-start | bytes 1572872 | tf_op jit(solution)/shard_map/ppermute | solution.py:80
  314.3 11.3 %collective-permute-start.24 = (bf16[128,2048]{1,0:T(8,128)(2,1)S(1)}, bf16[128,2048]{1,0:T(8,128)(2,1)S(1)}, u32[]{:S(2)}, u32[]{:S(2)}) collective-permute-start(bf16[128,2048]{1,0:T(8,128)(2,1)S(1)} %collective-permute-done.23), channel_id=1, source_target_pairs={{0,1},{1,0},{2,3},{3,2},{4,5},{5,4},{6,7},{7,6},{8,9},{9,8},{10,11... | collective-permute-start | bytes 1572872 | tf_op jit(solution)/shard_map/ppermute | solution.py:80
  314.4 28.0 %collective-permute-start.4 = (bf16[256,1536]{1,0:T(8,128)(2,1)S(1)}, bf16[256,1536]{1,0:T(8,128)(2,1)S(1)}, u32[]{:S(2)}, u32[]{:S(2)}) collective-permute-start(bf16[256,1536]{1,0:T(8,128)(2,1)S(1)} %collective-permute-done.3), channel_id=1, source_target_pairs={{0,8},{4,12},{8,16},{12,20},{16,24},{20,28},{24,0},{28,4},{1,9},{5... | collective-permute-start | bytes 2359304 | tf_op jit(solution)/shard_map/ppermute | solution.py:51
  325.5 28.1 %collective-permute-start.29 = (bf16[128,2048]{1,0:T(8,128)(2,1)S(1)}, bf16[128,2048]{1,0:T(8,128)(2,1)S(1)}, u32[]{:S(2)}, u32[]{:S(2)}) collective-permute-start(bf16[128,2048]{1,0:T(8,128)(2,1)S(1)} %collective-permute-done.27), channel_id=1, source_target_pairs={{0,8},{4,12},{8,16},{12,20},{16,24},{20,28},{24,0},{28,4},{1,9},{5... | collective-permute-start | bytes 1572872 | tf_op jit(solution)/shard_map/ppermute | solution.py:51
  325.5 28.1 %collective-permute-start.28 = (bf16[128,2048]{1,0:T(8,128)(2,1)S(1)}, bf16[128,2048]{1,0:T(8,128)(2,1)S(1)}, u32[]{:S(2)}, u32[]{:S(2)}) collective-permute-start(bf16[128,2048]{1,0:T(8,128)(2,1)S(1)} %collective-permute-done.27), channel_id=1, source_target_pairs={{0,1},{1,0},{2,3},{3,2},{4,5},{5,4},{6,7},{7,6},{8,9},{9,8},{10,11... | collective-permute-start | bytes 1572872 | tf_op jit(solution)/shard_map/ppermute | solution.py:80
  342.4 37.8 %collective-permute-start.5 = (bf16[256,1536]{1,0:T(8,128)(2,1)S(1)}, bf16[256,1536]{1,0:T(8,128)(2,1)S(1)}, u32[]{:S(2)}, u32[]{:S(2)}) collective-permute-start(bf16[256,1536]{1,0:T(8,128)(2,1)S(1)} %collective-permute-done.4), channel_id=1, source_target_pairs={{0,8},{4,12},{8,16},{12,20},{16,24},{20,28},{24,0},{28,4},{1,9},{5... | collective-permute-start | bytes 2359304 | tf_op jit(solution)/shard_map/ppermute | solution.py:51
  381.3 20.4 %collective-permute-start.6 = (bf16[256,1536]{1,0:T(8,128)(2,1)S(1)}, bf16[256,1536]{1,0:T(8,128)(2,1)S(1)}, u32[]{:S(2)}, u32[]{:S(2)}) collective-permute-start(bf16[256,1536]{1,0:T(8,128)(2,1)S(1)} %convolution_convert_fusion), channel_id=1, source_target_pairs={{0,4},{4,0},{8,12},{12,8},{16,20},{20,16},{24,28},{28,24},{1,5},{5... | collective-permute-start | bytes 2359304 | tf_op jit(solution)/shard_map/ppermute | solution.py:59
  383.9 40.3 %collective-permute-start.32 = (bf16[256,2048]{1,0:T(8,128)(2,1)S(1)}, bf16[256,2048]{1,0:T(8,128)(2,1)S(1)}, u32[]{:S(2)}, u32[]{:S(2)}) collective-permute-start(bf16[256,2048]{1,0:T(8,128)(2,1)S(1)} %fusion.8), channel_id=1, source_target_pairs={{0,4},{4,0},{8,12},{12,8},{16,20},{20,16},{24,28},{28,24},{1,5},{5... | collective-permute-start | bytes 3145736 | tf_op jit(solution)/shard_map/ppermute | solution.py:59
  386.4 60.2 %collective-permute-start.31 = (bf16[256,2048]{1,0:T(8,128)(2,1)S(1)}, bf16[256,2048]{1,0:T(8,128)(2,1)S(1)}, u32[]{:S(2)}, u32[]{:S(2)}) collective-permute-start(bf16[256,2048]{1,0:T(8,128)(2,1)S(1)} %fusion.7), channel_id=1, source_target_pairs={{0,4},{4,0},{8,12},{12,8},{16,20},{20,16},{24,28},{28,24},{1,5},{5... | collective-permute-start | bytes 3145736 | tf_op jit(solution)/shard_map/ppermute | solution.py:59
  388.8 79.5 %collective-permute-start.33 = (bf16[2048,256]{1,0:T(8,128)(2,1)S(1)}, bf16[2048,256]{1,0:T(8,128)(2,1)S(1)}, u32[]{:S(2)}, u32[]{:S(2)}) collective-permute-start(bf16[2048,256]{1,0:T(8,128)(2,1)S(1)} %fusion.9), channel_id=1, source_target_pairs={{0,4},{4,0},{8,12},{12,8},{16,20},{20,16},{24,28},{28,24},{1,5},{5... | collective-permute-start | bytes 3145736 | tf_op jit(solution)/shard_map/ppermute | solution.py:59
  (37 other events, 466.5 us)
